TPU v7x, 16 devices: a whole 2x2x2 slice. The times are simulated.
16 devices in a mesh: data: 4 (over z, y), seq: 4 (over x, core).
Axes of the slice: x: 2, y: 2, z: 2, core: 2. Of those that a mesh axis runs over, the one named last changes fastest.
Arguments:
- x_in: bfloat16 [16, 2048, 2048], P(None, ('data', 'seq')), parts along dimension 1
- positions: int32 [2048], P(('data', 'seq')), parts along dimension 0
- w_query: bfloat16 [3, 2048, 32, 64], replicated
- w_key: bfloat16 [3, 2048, 4, 64], replicated
- w_value: bfloat16 [3, 2048, 4, 64], replicated
- w_out: bfloat16 [3, 32, 64, 2048], replicated
- w_up: bfloat16 [3, 2048, 5632], replicated
- w_down: bfloat16 [3, 5632, 2048], replicated
- g_attn: float32 [3, 2048], replicated
- g_mlp: float32 [3, 2048], replicated
Outputs:
- output: bfloat16 [16, 2048, 2048], P(None, ('data', 'seq')), parts along dimension 1
There are 4 independent parts. A program takes and returns all parts, laid end to end along the dimension named above; an argument that names none is the same for every part.
All inputs are finite; a program needn't handle non-finite values.
Results may differ from a plain program's by a relative error of at most 0.0166372.
Values are sent between devices in bfloat16 or wider.
A program may use at most 1 GiB of HBM per device.

v0:
```python
import jax
import jax.numpy as jnp
from jax import lax
from jax.sharding import PartitionSpec as P

ROPE_BASE = 10000.0
NORM_EPS = 1e-6


def rms_norm(x_act, gain_vec):
    x_f32 = x_act.astype(jnp.float32)
    mean_sq = jnp.mean(x_f32 * x_f32, axis=-1, keepdims=True)
    return (x_f32 * lax.rsqrt(mean_sq + NORM_EPS) * gain_vec).astype(jnp.bfloat16)


def rope_tables(positions, head_dim):
    inv_freq = ROPE_BASE ** (-jnp.arange(head_dim // 2, dtype=jnp.float32) * (2.0 / head_dim))
    angles = positions.astype(jnp.float32)[..., None] * inv_freq
    return jnp.cos(angles), jnp.sin(angles)


def apply_rope(proj_f32, cos_t, sin_t):
    half_dim = proj_f32.shape[-1] // 2
    x_first = proj_f32[..., :half_dim]
    x_second = proj_f32[..., half_dim:]
    cos_b = cos_t[..., None, :]
    sin_b = sin_t[..., None, :]
    return jnp.concatenate([x_first * cos_b - x_second * sin_b, x_second * cos_b + x_first * sin_b], axis=-1).astype(jnp.bfloat16)


def causal_attention(q_heads, k_heads, v_heads, q_offset, q_block):
    n_batch, q_len, kv_heads, groups, head_dim = q_heads.shape
    key_len = k_heads.shape[1]
    n_blocks = q_len // q_block
    att_scale = head_dim ** -0.5
    key_pos = jnp.arange(key_len)

    def one_block(blk_idx):
        blk_start = blk_idx * q_block
        q_blk = lax.dynamic_slice_in_dim(q_heads, blk_start, q_block, axis=1)
        scores = jnp.einsum("bqkgd,bskd->bkgqs", q_blk, k_heads, preferred_element_type=jnp.float32) * att_scale
        query_pos = q_offset + blk_start + jnp.arange(q_block)
        scores = jnp.where(key_pos[None, :] <= query_pos[:, None], scores, -1e30)
        row_max = jnp.max(scores, axis=-1, keepdims=True)
        exp_f32 = jnp.exp(scores - row_max)
        row_sum = jnp.sum(exp_f32, axis=-1)
        weighted = jnp.einsum("bkgqs,bskd->bqkgd", exp_f32.astype(jnp.bfloat16), v_heads, preferred_element_type=jnp.float32)
        return (weighted / jnp.transpose(row_sum, (0, 3, 1, 2))[..., None]).astype(jnp.bfloat16)

    blocks = lax.map(one_block, jnp.arange(n_blocks))
    return jnp.moveaxis(blocks, 0, 1).reshape(n_batch, q_len, kv_heads * groups, head_dim)


def layer_step(hidden, cos_t, sin_t, w_query, w_key, w_value, w_out, w_up, w_down, gain_attn, gain_mlp):
    normed = rms_norm(hidden, gain_attn)
    q_loc = apply_rope(jnp.einsum("bsd,dhe->bshe", normed, w_query, preferred_element_type=jnp.float32), cos_t, sin_t)
    k_loc = apply_rope(jnp.einsum("bsd,dhe->bshe", normed, w_key, preferred_element_type=jnp.float32), cos_t, sin_t)
    v_loc = jnp.einsum("bsd,dhe->bshe", normed, w_value, preferred_element_type=jnp.float32).astype(jnp.bfloat16)
    q_all = lax.all_to_all(q_loc, "seq", 2, 1, tiled=True)
    k_all = lax.all_to_all(k_loc, "seq", 2, 1, tiled=True)
    v_all = lax.all_to_all(v_loc, "seq", 2, 1, tiled=True)
    n_batch, seq_len, heads_loc, head_dim = q_all.shape
    kv_loc = k_all.shape[2]
    q_grouped = q_all.reshape(n_batch, seq_len, kv_loc, heads_loc // kv_loc, head_dim)
    attn_heads = causal_attention(q_grouped, k_all, v_all, 0, min(256, seq_len))
    attn_loc = lax.all_to_all(attn_heads, "seq", 1, 2, tiled=True)
    resid_h = (hidden.astype(jnp.float32) + jnp.einsum("bshe,hed->bsd", attn_loc, w_out, preferred_element_type=jnp.float32)).astype(jnp.bfloat16)
    normed_mlp = rms_norm(resid_h, gain_mlp)
    gelu_act = jax.nn.gelu(jnp.einsum("bsd,df->bsf", normed_mlp, w_up, preferred_element_type=jnp.float32), approximate=True).astype(jnp.bfloat16)
    layer_out = resid_h.astype(jnp.float32) + jnp.einsum("bsf,fd->bsd", gelu_act, w_down, preferred_element_type=jnp.float32)
    return layer_out.astype(jnp.bfloat16)


def solution(mesh):
    tok_spec = P(None, ("data", "seq"), None)
    in_specs = (tok_spec, P(("data", "seq"))) + (P(),) * 8

    def device_fn(x_loc, pos_loc, w_query, w_key, w_value, w_out, w_up, w_down, g_attn, g_mlp):
        cos_t, sin_t = rope_tables(pos_loc, w_query.shape[-1])
        hidden = x_loc
        for layer_idx in range(w_query.shape[0]):
            hidden = layer_step(hidden, cos_t, sin_t, w_query[layer_idx], w_key[layer_idx], w_value[layer_idx], w_out[layer_idx], w_up[layer_idx], w_down[layer_idx], g_attn[layer_idx], g_mlp[layer_idx])
        return hidden

    return jax.shard_map(device_fn, mesh=mesh, in_specs=in_specs, out_specs=tok_spec, check_vma=False)
```

profile of v0, /device:TPU:7, one launch (start us, length us, event | category | flops | bytes accessed | tf_op | source)
XLA Modules:
  0.0 2088.5 jit_solution(12445892430977786244)
XLA Ops:
  89.7 89.9 %all-to-all-done = bf16[16,128,32,64]{1,3,0,2:T(8,128)(2,1)} async-done(((bf16[16,128,32,64]{1,3,0,2:T(8,128)(2,1)}), bf16[16,128,32,64]{1,3,0,2:T(8,128)(2,1)}, u32[]{:S(2)}, u32[]{:S(2)}) %all-to-all-start) | async-done | bytes 8388640 | tf_op jit(solution)/shard_map/all_to_all | solution.py:59
  208.5 151.5 %while.33 = (s32[]{:T(128)}, bf16[2,16,256,1,8,64]{2,5,4,1,3,0:T(8,128)(2,1)}, s32[2]{0:T(128)S(1)}, bf16[16,512,1,8,64]{1,4,3,0,2:T(8,128)(2,1)}, bf16[16,512,1...) while((s32[]{:T(128)}, ...), condition=%wide.region_4.5_spmd.clone, body=%wide.region_1.4_spmd.clone.sunk | while | flops 4483776512 | bytes 212994720 | solution.py:50
  210.0 26.4 %fusion.319 = (f32[16,8,256]{2,1,0:T(8,128)S(1)}, f32[16,256,8,512]{3,1,2,0:T(8,128)}) fusion(pred[256,512]{1,0:T(8,128)(4,1)S(1)} %iota_compare_fusion.6, bf16[16,512,1,64]{1,3,0,2:T(8,128)(2,1)S(1)} %get-tuple-element.380, bf16[16,512,1,8,64]{1,4,3,0,2:T(8,128)(2,1)} %get-tuple-element.379, s32[]{:T(128)S(6)} %select_n.76), kind=kOutput, calls=%fused_computation.7.clone.1 | convolution fusion | flops 2197782528 | bytes 72613888 | tf_op jit(solution)/shard_map/while/body/eval_jaxpr/bqkgd,bskd->bkgqs/dot_general | solution.py:41
  257.9 26.3 %bitcast_dynamic-update-slice_fusion.6 = bf16[2,16,256,1,8,64]{2,5,4,1,3,0:T(8,128)(2,1)} fusion(bf16[2,16,256,1,8,64]{2,5,4,1,3,0:T(8,128)(2,1)} %get-tuple-element.367, s32[]{:T(128)} %get-tuple-element.366, f32[16,256,8]{1,2,0:T(8,128)S(1)} %bitcast.519, f32[16,256,8,512]{3,1,2,0:T(8,128)} %get-tuple-element.338, ...), kind=kOutput, calls=%fused_computation.13.clone.1 | convolution fusion | flops 2218786816 | bytes 72745472 | tf_op jit(solution)/shard_map/while/body/eval_jaxpr/bkgqs,bskd->bqkgd/dot_general | solution.py:47
  285.7 26.4 %fusion.319 = (f32[16,8,256]{2,1,0:T(8,128)S(1)}, f32[16,256,8,512]{3,1,2,0:T(8,128)}) fusion(pred[256,512]{1,0:T(8,128)(4,1)S(1)} %iota_compare_fusion.6, bf16[16,512,1,64]{1,3,0,2:T(8,128)(2,1)S(1)} %get-tuple-element.380, bf16[16,512,1,8,64]{1,4,3,0,2:T(8,128)(2,1)} %get-tuple-element.379, s32[]{:T(128)S(6)} %select_n.76), kind=kOutput, calls=%fused_computation.7.clone.1 | convolution fusion | flops 2197782528 | bytes 72613888 | tf_op jit(solution)/shard_map/while/body/eval_jaxpr/bqkgd,bskd->bkgqs/dot_general | solution.py:41
  360.0 33.3 %copy.71 = bf16[16,2,256,1,8,64]{5,4,0,2,1,3:T(8,128)(2,1)} copy(bf16[16,2,256,1,8,64]{2,5,4,0,3,1:T(8,128)(2,1)} %bitcast.511) | data formatting | bytes 16777216 | tf_op jit(solution)/shard_map/reshape | solution.py:51
  417.9 90.5 %all-to-all-done.3 = bf16[4,2,524288]{2,1,0:T(2,128)(2,1)} async-done(((bf16[4,2,524288]{2,1,0:T(2,128)(2,1)}), bf16[4,2,524288]{2,1,0:T(2,128)(2,1)}, u32[]{:S(2)}, u32[]{:S(2)}) %all-to-all-start.3) | async-done | bytes 8388640 | tf_op jit(solution)/shard_map/all_to_all | solution.py:66
  578.1 62.6 %fusion.185.clone.5 = bf16[16,128,5632]{2,1,0:T(8,128)(2,1)} fusion(bf16[3,2048,5632]{2,1,0:T(8,128)(2,1)} %param.22, bf16[16,128,2048]{2,1,0:T(8,128)(2,1)} %get-tuple-element.224, f32[2048]{0:T(1024)S(1)} %bitcast.533, f32[16,128]{1,0:T(8,128)S(1)} %add_rsqrt_fusion.4), kind=kOutput, calls=%fused_computation.76.clone.clone.clone.clone.clone.clone.2 | convolution fusion | flops 47365226496 | bytes 54542336 | tf_op jit(solution)/shard_map/bsd,df->bsf/dot_general | solution.py:69
  640.7 61.3 %fusion.130 = (f32[16,128]{1,0:T(8,128)S(1)}, bf16[16,128,2048]{2,1,0:T(8,128)(2,1)}) fusion(bf16[3,5632,2048]{2,1,0:T(8,128)(2,1)} %param.23, bf16[16,128,2048]{2,1,0:T(8,128)(2,1)} %get-tuple-element.224, bf16[16,128,5632]{2,1,0:T(8,128)(2,1)} %fusion.185.clone.5), kind=kOutput, calls=%fused_computation.146 | convolution fusion | flops 47269806080 | bytes 62922752 | tf_op jit(solution)/shard_map/bsf,fd->bsd/dot_general | solution.py:70
  790.1 90.8 %all-to-all-done.4 = bf16[16,128,32,64]{1,3,0,2:T(8,128)(2,1)} async-done(((bf16[16,128,32,64]{1,3,0,2:T(8,128)(2,1)}), bf16[16,128,32,64]{1,3,0,2:T(8,128)(2,1)}, u32[]{:S(2)}, u32[]{:S(2)}) %all-to-all-start.4) | async-done | bytes 8388640 | tf_op jit(solution)/shard_map/all_to_all | solution.py:59
  909.7 151.5 %while.34 = (s32[]{:T(128)}, bf16[2,16,256,1,8,64]{2,5,4,1,3,0:T(8,128)(2,1)}, s32[2]{0:T(128)S(1)}, bf16[16,512,1,8,64]{1,4,3,0,2:T(8,128)(2,1)}, bf16[16,512,1...) while((s32[]{:T(128)}, ...), condition=%wide.region_10.11_spmd.clone, body=%wide.region_7.10_spmd.clone.sunk | while | flops 4483776512 | bytes 212994720 | solution.py:50
  911.2 26.4 %fusion.323 = (f32[16,8,256]{2,1,0:T(8,128)S(1)}, f32[16,256,8,512]{3,1,2,0:T(8,128)}) fusion(pred[256,512]{1,0:T(8,128)(4,1)S(1)} %iota_compare_fusion.7, bf16[16,512,1,64]{1,3,0,2:T(8,128)(2,1)S(1)} %get-tuple-element.410, bf16[16,512,1,8,64]{1,4,3,0,2:T(8,128)(2,1)} %get-tuple-element.409, s32[]{:T(128)S(6)} %select_n.80), kind=kOutput, calls=%fused_computation.28.clone.1 | convolution fusion | flops 2197782528 | bytes 72613888 | tf_op jit(solution)/shard_map/while/body/eval_jaxpr/bqkgd,bskd->bkgqs/dot_general | solution.py:41
  959.1 26.3 %bitcast_dynamic-update-slice_fusion.7 = bf16[2,16,256,1,8,64]{2,5,4,1,3,0:T(8,128)(2,1)} fusion(bf16[2,16,256,1,8,64]{2,5,4,1,3,0:T(8,128)(2,1)} %get-tuple-element.397, s32[]{:T(128)} %get-tuple-element.396, f32[16,256,8]{1,2,0:T(8,128)S(1)} %bitcast.520, f32[16,256,8,512]{3,1,2,0:T(8,128)} %get-tuple-element.346, ...), kind=kOutput, calls=%fused_computation.34.clone.1 | convolution fusion | flops 2218786816 | bytes 72745472 | tf_op jit(solution)/shard_map/while/body/eval_jaxpr/bkgqs,bskd->bqkgd/dot_general | solution.py:47
  986.9 26.4 %fusion.323 = (f32[16,8,256]{2,1,0:T(8,128)S(1)}, f32[16,256,8,512]{3,1,2,0:T(8,128)}) fusion(pred[256,512]{1,0:T(8,128)(4,1)S(1)} %iota_compare_fusion.7, bf16[16,512,1,64]{1,3,0,2:T(8,128)(2,1)S(1)} %get-tuple-element.410, bf16[16,512,1,8,64]{1,4,3,0,2:T(8,128)(2,1)} %get-tuple-element.409, s32[]{:T(128)S(6)} %select_n.80), kind=kOutput, calls=%fused_computation.28.clone.1 | convolution fusion | flops 2197782528 | bytes 72613888 | tf_op jit(solution)/shard_map/while/body/eval_jaxpr/bqkgd,bskd->bkgqs/dot_general | solution.py:41
  1101.9 100.3 %all_to_all.207 = bf16[4,2,524288]{2,1,0:T(2,128)(2,1)} all-to-all(bf16[4,2,524288]{2,1,0:T(2,128)(2,1)} %reshape.278), channel_id=1, replica_groups=mesh['data'=4,'seq'=4] {'seq'}, dimensions={0} | all-to-all | bytes 16777216 | tf_op jit(solution)/shard_map/all_to_all | solution.py:66
  1272.0 62.6 %fusion.201.clone.5 = bf16[16,128,5632]{2,1,0:T(8,128)(2,1)} fusion(bf16[3,2048,5632]{2,1,0:T(8,128)(2,1)} %param.22, bf16[16,128,2048]{2,1,0:T(8,128)(2,1)} %get-tuple-element.228, f32[2048]{0:T(1024)S(1)} %bitcast.529, f32[16,128]{1,0:T(8,128)S(1)} %add_rsqrt_fusion.2), kind=kOutput, calls=%fused_computation.84.clone.clone.clone.clone.clone.clone.2 | convolution fusion | flops 47365226496 | bytes 54542336 | tf_op jit(solution)/shard_map/bsd,df->bsf/dot_general | solution.py:69
  1334.6 61.3 %fusion.138 = (f32[16,128]{1,0:T(8,128)S(1)}, bf16[16,128,2048]{2,1,0:T(8,128)(2,1)}) fusion(bf16[3,5632,2048]{2,1,0:T(8,128)(2,1)} %param.23, bf16[16,128,2048]{2,1,0:T(8,128)(2,1)} %get-tuple-element.228, bf16[16,128,5632]{2,1,0:T(8,128)(2,1)} %fusion.201.clone.5), kind=kOutput, calls=%fused_computation.154 | convolution fusion | flops 47269806080 | bytes 62922752 | tf_op jit(solution)/shard_map/bsf,fd->bsd/dot_general | solution.py:70
  1484.0 90.8 %all-to-all-done.8 = bf16[16,128,32,64]{1,3,0,2:T(8,128)(2,1)} async-done(((bf16[16,128,32,64]{1,3,0,2:T(8,128)(2,1)}), bf16[16,128,32,64]{1,3,0,2:T(8,128)(2,1)}, u32[]{:S(2)}, u32[]{:S(2)}) %all-to-all-start.8) | async-done | bytes 8388640 | tf_op jit(solution)/shard_map/all_to_all | solution.py:59
  1603.6 151.5 %while.35 = (s32[]{:T(128)}, bf16[2,16,256,1,8,64]{2,5,4,1,3,0:T(8,128)(2,1)}, s32[2]{0:T(128)S(1)}, bf16[16,512,1,8,64]{1,4,3,0,2:T(8,128)(2,1)}, bf16[16,512,1...) while((s32[]{:T(128)}, ...), condition=%wide.region_16.17_spmd.clone, body=%wide.region_13.16_spmd.clone.sunk | while | flops 4483776512 | bytes 212994720 | solution.py:50
  1605.1 26.4 %fusion.327 = (f32[16,8,256]{2,1,0:T(8,128)S(1)}, f32[16,256,8,512]{3,1,2,0:T(8,128)}) fusion(pred[256,512]{1,0:T(8,128)(4,1)S(1)} %iota_compare_fusion.8, bf16[16,512,1,64]{1,3,0,2:T(8,128)(2,1)S(1)} %get-tuple-element.440, bf16[16,512,1,8,64]{1,4,3,0,2:T(8,128)(2,1)} %get-tuple-element.439, s32[]{:T(128)S(6)} %select_n.84), kind=kOutput, calls=%fused_computation.49.clone.1 | convolution fusion | flops 2197782528 | bytes 72613888 | tf_op jit(solution)/shard_map/while/body/eval_jaxpr/bqkgd,bskd->bkgqs/dot_general | solution.py:41
  1680.8 26.4 %fusion.327 = (f32[16,8,256]{2,1,0:T(8,128)S(1)}, f32[16,256,8,512]{3,1,2,0:T(8,128)}) fusion(pred[256,512]{1,0:T(8,128)(4,1)S(1)} %iota_compare_fusion.8, bf16[16,512,1,64]{1,3,0,2:T(8,128)(2,1)S(1)} %get-tuple-element.440, bf16[16,512,1,8,64]{1,4,3,0,2:T(8,128)(2,1)} %get-tuple-element.439, s32[]{:T(128)S(6)} %select_n.84), kind=kOutput, calls=%fused_computation.49.clone.1 | convolution fusion | flops 2197782528 | bytes 72613888 | tf_op jit(solution)/shard_map/while/body/eval_jaxpr/bqkgd,bskd->bkgqs/dot_general | solution.py:41
  1795.7 100.3 %all_to_all.208 = bf16[4,2,524288]{2,1,0:T(2,128)(2,1)} all-to-all(bf16[4,2,524288]{2,1,0:T(2,128)(2,1)} %reshape.280), channel_id=1, replica_groups=mesh['data'=4,'seq'=4] {'seq'}, dimensions={0} | all-to-all | bytes 16777216 | tf_op jit(solution)/shard_map/all_to_all | solution.py:66
  1965.8 62.4 %fusion.303 = bf16[16,128,5632]{2,1,0:T(8,128)(2,1)} fusion(bf16[3,2048,5632]{2,1,0:T(8,128)(2,1)} %param.22, bf16[16,128,2048]{2,1,0:T(8,128)(2,1)} %get-tuple-element.232, f32[2048]{0:T(1024)S(1)} %bitcast.525, f32[16,128]{1,0:T(8,128)S(1)} %add_rsqrt_fusion), kind=kOutput, calls=%fused_computation.92.clone.clone.clone.clone.2 | convolution fusion | flops 47365226496 | bytes 54542336 | tf_op jit(solution)/shard_map/bsd,df->bsf/dot_general | solution.py:69
  2028.2 59.9 %fusion.145 = bf16[16,128,2048]{2,1,0:T(8,128)(2,1)} fusion(bf16[16,128,2048]{2,1,0:T(8,128)(2,1)} %get-tuple-element.232, bf16[3,5632,2048]{2,1,0:T(8,128)(2,1)} %param.23, bf16[16,128,5632]{2,1,0:T(8,128)(2,1)} %fusion.303), kind=kOutput, calls=%fused_computation.161 | convolution fusion | flops 47257223168 | bytes 62914560 | tf_op jit(solution)/shard_map/bsf,fd->bsd/dot_general | solution.py:70
  (149 shorter events, 906.2 us)
Async XLA Ops:
  7.4 46.4 %copy-start.1 = (f32[128,32]{0,1:T(8,128)}, f32[128,32]{0,1:T(8,128)S(1)}, u32[]{:S(2)}) copy-start(f32[128,32]{0,1:T(8,128)S(1)} %get-tuple-element.221) | copy-start | bytes 49156
  7.4 46.4 %copy-start.4 = (f32[128,32]{0,1:T(8,128)}, f32[128,32]{0,1:T(8,128)S(1)}, u32[]{:S(2)}) copy-start(f32[128,32]{0,1:T(8,128)S(1)} %get-tuple-element.222) | copy-start | bytes 49156
  14.2 35.8 %all-to-all-start.1 = ((bf16[16,128,4,64]{1,3,0,2:T(8,128)(2,1)}), bf16[16,128,4,64]{1,3,0,2:T(8,128)(2,1)S(1)}, u32[]{:S(2)}, u32[]{:S(2)}) async-start(bf16[16,128,4,64]{1,3,0,2:T(8,128)(2,1)} %copy.31), calls=%async_computation.1 | async-start | bytes 2097152 | tf_op jit(solution)/shard_map/all_to_all | solution.py:60
  50.0 32.7 %all-to-all-start.2 = ((bf16[16,128,4,64]{1,3,0,2:T(8,128)(2,1)}), bf16[16,128,4,64]{1,3,0,2:T(8,128)(2,1)S(1)}, u32[]{:S(2)}, u32[]{:S(2)}) async-start(bf16[16,128,4,64]{1,3,0,2:T(8,128)(2,1)} %copy.33), calls=%async_computation.2 | async-start | bytes 2097152 | tf_op jit(solution)/shard_map/all_to_all | solution.py:61
  82.8 96.8 %all-to-all-start = ((bf16[16,128,32,64]{1,3,0,2:T(8,128)(2,1)}), bf16[16,128,32,64]{1,3,0,2:T(8,128)(2,1)}, u32[]{:S(2)}, u32[]{:S(2)}) async-start(bf16[16,128,32,64]{1,3,0,2:T(8,128)(2,1)} %copy.29), calls=%async_computation | async-start | bytes 16777216 | tf_op jit(solution)/shard_map/all_to_all | solution.py:59
  190.8 17.7 copy-start
  393.3 23.9 %copy-start.7 = (f32[3,2048]{1,0:T(4,128)S(1)}, f32[3,2048]{1,0:T(4,128)}, u32[]{:S(2)}) copy-start(f32[3,2048]{1,0:T(4,128)} %param.25) | copy-start | bytes 73732
  409.9 98.5 %all-to-all-start.3 = ((bf16[4,2,524288]{2,1,0:T(2,128)(2,1)}), bf16[4,2,524288]{2,1,0:T(2,128)(2,1)}, u32[]{:S(2)}, u32[]{:S(2)}) async-start(bf16[4,2,524288]{2,1,0:T(2,128)(2,1)} %reshape.276), calls=%async_computation.3 | async-start | bytes 16777216 | tf_op jit(solution)/shard_map/all_to_all | solution.py:66
  640.7 61.3 %copy-start.10 = (f32[1,2048]{1,0:T(1,128)S(1)}, f32[1,2048]{1,0:T(1,128)}, u32[]{:S(2)}) copy-start(f32[1,2048]{1,0:T(1,128)} %get-tuple-element.220) | copy-start | bytes 24580
  702.0 6.3 copy-start.13
  731.8 17.6 all-to-all-start.6
  737.1 5.3 copy-start.2
  737.1 5.3 copy-start.5
  749.4 34.2 %all-to-all-start.5 = ((bf16[16,128,4,64]{1,3,0,2:T(8,128)(2,1)}), bf16[16,128,4,64]{1,3,0,2:T(8,128)(2,1)S(1)}, u32[]{:S(2)}, u32[]{:S(2)}) async-start(bf16[16,128,4,64]{1,3,0,2:T(8,128)(2,1)} %copy.41), calls=%async_computation.5 | async-start | bytes 2097152 | tf_op jit(solution)/shard_map/all_to_all | solution.py:60
  783.7 97.2 %all-to-all-start.4 = ((bf16[16,128,32,64]{1,3,0,2:T(8,128)(2,1)}), bf16[16,128,32,64]{1,3,0,2:T(8,128)(2,1)}, u32[]{:S(2)}, u32[]{:S(2)}) async-start(bf16[16,128,32,64]{1,3,0,2:T(8,128)(2,1)} %copy.39), calls=%async_computation.4 | async-start | bytes 16777216 | tf_op jit(solution)/shard_map/all_to_all | solution.py:59
  1246.4 25.5 %copy-start.11 = (f32[1,2048]{1,0:T(1,128)S(1)}, f32[1,2048]{1,0:T(1,128)}, u32[]{:S(2)}) copy-start(f32[1,2048]{1,0:T(1,128)} %get-tuple-element.217) | copy-start | bytes 24580
  1334.6 61.3 %copy-start.8 = (f32[1,2048]{1,0:T(1,128)S(1)}, f32[1,2048]{1,0:T(1,128)}, u32[]{:S(2)}) copy-start(f32[1,2048]{1,0:T(1,128)} %get-tuple-element.218) | copy-start | bytes 24580
  1395.9 6.3 copy-start.12
  1425.7 17.6 all-to-all-start.10
  1431.0 5.3 copy-start.3
  1431.0 5.3 copy-start.6
  1443.3 34.2 %all-to-all-start.9 = ((bf16[16,128,4,64]{1,3,0,2:T(8,128)(2,1)}), bf16[16,128,4,64]{1,3,0,2:T(8,128)(2,1)S(1)}, u32[]{:S(2)}, u32[]{:S(2)}) async-start(bf16[16,128,4,64]{1,3,0,2:T(8,128)(2,1)} %copy.51), calls=%async_computation.9 | async-start | bytes 2097152 | tf_op jit(solution)/shard_map/all_to_all | solution.py:60
  1477.6 97.2 %all-to-all-start.8 = ((bf16[16,128,32,64]{1,3,0,2:T(8,128)(2,1)}), bf16[16,128,32,64]{1,3,0,2:T(8,128)(2,1)}, u32[]{:S(2)}, u32[]{:S(2)}) async-start(bf16[16,128,32,64]{1,3,0,2:T(8,128)(2,1)} %copy.49), calls=%async_computation.8 | async-start | bytes 16777216 | tf_op jit(solution)/shard_map/all_to_all | solution.py:59
  1940.3 25.5 %copy-start.9 = (f32[1,2048]{1,0:T(1,128)S(1)}, f32[1,2048]{1,0:T(1,128)}, u32[]{:S(2)}) copy-start(f32[1,2048]{1,0:T(1,128)} %get-tuple-element.215) | copy-start | bytes 24580
where the time goes:
time: 2100 us; the launch traced here: 2090 us
  matrix products  867 us (41%)
  local copies, waits for them, and re-layouts  394 us (19%)
  waiting for transfers between devices  373 us (18%)
  blocking collectives  201 us (10%)
  other arithmetic  195 us (9%)
  starting transfers between devices  54.5 us (3%)
    all_to_all x3, waiting for transfers between devices, layer_step(): q_all = lax.all_to_all(q_loc, 'seq', 2, 1, tiled=True)  271 us
    all_to_all x2, blocking collectives, layer_step(): attn_loc = lax.all_to_all(attn_heads, 'seq', 1, 2, tiled=True)  201 us
    dot_general x3, matrix products, layer_step(): jnp.einsum('bsd,df->bsf', normed_mlp, w_up, preferred_element_type=jnp.fl...  188 us
    dot_general x3, matrix products, layer_step(): jnp.einsum('bsf,fd->bsd', gelu_act, w_down, preferred_element_type=jnp.fl...  182 us
    dot_general x6, matrix products, one_block(): jnp.einsum('bqkgd,bskd->bkgqs', q_blk, k_heads, preferred_element_type=jn...  159 us
    dot_general x6, matrix products, one_block(): jnp.einsum('bkgqs,bskd->bqkgd', exp_f32.astype(jnp.bfloat16), v_heads, pr...  158 us
    reduce_sum x6, other arithmetic, one_block(): row_sum = jnp.sum(exp_f32, axis=-1)  129 us
    unnamed x34, local copies, waits for them, and re-layouts  97.6 us
  transfers between devices with their start and end apart: 10, of which 6 were waited for; matrix products, arithmetic and copies ran while one was open for 6% of the time, Pallas kernels for 0%

commit v1 on v0

v1 whole, which is shorter than its diff:
```python
import functools

import jax
import jax.numpy as jnp
from jax import lax
from jax.experimental import pallas as pl
from jax.experimental.pallas import tpu as pltpu
from jax.sharding import PartitionSpec as P

ROPE_BASE = 10000.0
NORM_EPS = 1e-6
LOG2E = 1.4426950408889634
F32 = jnp.float32
BF16 = jnp.bfloat16
NT = (((1,), (1,)), ((), ()))
VMEM_LIMIT = 64 * 1024 * 1024 - 65536


def params(limit=VMEM_LIMIT):
    return pltpu.CompilerParams(dimension_semantics=("arbitrary",), vmem_limit_bytes=limit)


def cost(flops, nbytes):
    return pl.CostEstimate(flops=int(flops), bytes_accessed=int(nbytes), transcendentals=0)


def normed(x_bf16, gain):
    x = x_bf16.astype(F32)
    mean_sq = jnp.mean(x * x, axis=-1, keepdims=True)
    return (x * lax.rsqrt(mean_sq + NORM_EPS) * gain).astype(BF16)


def rope_t(u, cos, sin):
    half = u.shape[0] // 2
    a, b = u[:half], u[half:]
    return jnp.concatenate([a * cos - b * sin, b * cos + a * sin], axis=0).astype(BF16)


def kv_body(head_dim, batch_rows, x_ref, g_ref, wk_ref, wv_ref, cos_ref, sin_ref, n_ref, k_ref, v_ref):
    n = normed(x_ref[...], g_ref[0])
    n_ref[...] = n
    k_t = lax.dot_general(wk_ref[0], n, NT, preferred_element_type=F32)
    v_t = lax.dot_general(wv_ref[0], n, NT, preferred_element_type=F32).astype(BF16)
    for i in range(n.shape[0] // batch_rows):
        cols = slice(i * batch_rows, (i + 1) * batch_rows)
        heads = [rope_t(k_t[h:h + head_dim, cols], cos_ref[...], sin_ref[...]) for h in range(0, k_t.shape[0], head_dim)]
        k_ref[i] = jnp.concatenate(heads, axis=0).T
        v_ref[i] = v_t[:, cols]


def kv_proj(layer, x, gain, wk, wv, cos, sin, head_dim, n_batch, tile=256):
    rows, d = x.shape
    kv = wk.shape[1]
    s = rows // n_batch
    per = tile // s
    return pl.pallas_call(
        functools.partial(kv_body, head_dim, s),
        grid=(rows // tile,),
        in_specs=[
            pl.BlockSpec((tile, d), lambda i: (i, 0)),
            pl.BlockSpec((1, 1, d), lambda i: (layer, 0, 0)),
            pl.BlockSpec((1, kv, d), lambda i: (layer, 0, 0)),
            pl.BlockSpec((1, kv, d), lambda i: (layer, 0, 0)),
            pl.BlockSpec(cos.shape, lambda i: (0, 0)),
            pl.BlockSpec(cos.shape, lambda i: (0, 0)),
        ],
        out_specs=[
            pl.BlockSpec((tile, d), lambda i: (i, 0)),
            pl.BlockSpec((per, s, kv), lambda i: (i, 0, 0)),
            pl.BlockSpec((per, kv, s), lambda i: (i, 0, 0)),
        ],
        out_shape=[
            jax.ShapeDtypeStruct((rows, d), BF16),
            jax.ShapeDtypeStruct((n_batch, s, kv), BF16),
            jax.ShapeDtypeStruct((n_batch, kv, s), BF16),
        ],
        compiler_params=params(),
        cost_estimate=cost(4 * rows * d * kv, 4 * rows * d),
        name=f"kv_proj",
    )(x, gain, wk, wv, cos, sin)


def q_body(head_dim, batch_rows, fchunk, n_ref, wq_ref, cos_ref, sin_ref, q_ref):
    feats = wq_ref.shape[1]
    for f0 in range(0, feats, fchunk):
        u = lax.dot_general(wq_ref[0, f0:f0 + fchunk, :], n_ref[...], NT, preferred_element_type=F32)
        for i in range(n_ref.shape[0] // batch_rows):
            cols = slice(i * batch_rows, (i + 1) * batch_rows)
            for h in range(0, fchunk, head_dim):
                q_ref[i, f0 + h:f0 + h + head_dim, :] = rope_t(u[h:h + head_dim, cols], cos_ref[...], sin_ref[...])


def q_proj(layer, n, wq, cos, sin, head_dim, n_batch, tile=256, fchunk=512):
    rows, d = n.shape
    feats = wq.shape[1]
    s = rows // n_batch
    per = tile // s
    return pl.pallas_call(
        functools.partial(q_body, head_dim, s, fchunk),
        grid=(rows // tile,),
        in_specs=[
            pl.BlockSpec((tile, d), lambda i: (i, 0)),
            pl.BlockSpec((1, feats, d), lambda i: (layer, 0, 0), pipeline_mode=pl.Buffered(1)),
            pl.BlockSpec(cos.shape, lambda i: (0, 0)),
            pl.BlockSpec(cos.shape, lambda i: (0, 0)),
        ],
        out_specs=pl.BlockSpec((per, feats, s), lambda i: (i, 0, 0)),
        out_shape=jax.ShapeDtypeStruct((n_batch, feats, s), BF16),
        compiler_params=params(),
        cost_estimate=cost(2 * rows * d * feats, 4 * rows * d + 2 * feats * d),
        name="q_proj",
    )(n, wq, cos, sin)


def attn_one(head_dim, n_kv, chunk, q_ref, k_refs, v_refs, o_ref):
    s = q_ref.shape[2]
    groups = q_ref.shape[1] // head_dim // n_kv
    factor = LOG2E * head_dim ** -0.5
    row = lax.broadcasted_iota(jnp.int32, (s, chunk * s), 0)
    col = lax.broadcasted_iota(jnp.int32, (s, chunk * s), 1) % s
    allowed = row <= col
    zeros = jnp.zeros((head_dim, chunk * s), BF16)
    pack = 128 // head_dim
    for g in range(n_kv):
        lanes = slice(g // pack * 128, g // pack * 128 + 128)
        k_all = jnp.concatenate([r[0, :, lanes] for r in k_refs], axis=0)
        v_all = jnp.concatenate([r[0, g * head_dim:(g + 1) * head_dim, :] for r in v_refs], axis=1)
        for c in range(groups // chunk):
            h0 = g * groups + c * chunk
            q = jnp.concatenate([q_ref[0, h * head_dim:(h + 1) * head_dim, :] for h in range(h0, h0 + chunk)], axis=1)
            q = jnp.concatenate([q if j == g % pack else zeros for j in range(pack)], axis=0)
            sc = jnp.dot(k_all, q, preferred_element_type=F32)
            full = sc.shape[0] - s
            diag = jnp.where(allowed, sc[full:], -jnp.inf)
            m = jnp.max(diag, axis=0, keepdims=True)
            if full:
                m = jnp.maximum(m, jnp.max(sc[:full], axis=0, keepdims=True))
                sc = jnp.concatenate([sc[:full], diag], axis=0)
            else:
                sc = diag
            e = jnp.exp2((sc - m) * factor)
            l = jnp.sum(e, axis=0, keepdims=True)
            o = jnp.dot(v_all, e.astype(BF16), preferred_element_type=F32) / l
            for h in range(0, chunk, pack):
                stacked = jnp.concatenate([o[:, (h + j) * s:(h + j + 1) * s] for j in range(pack)], axis=0)
                o_ref[0, :, (h0 + h) * head_dim:(h0 + h + pack) * head_dim] = stacked.astype(BF16).T


def attn_body(head_dim, n_kv, chunk, me_ref, q_ref, k0, v0, ka, va, kb, vb, kc, vc, o_ref):
    me = me_ref[0]
    k_sets = {0: [k0], 1: [kc, k0], 2: [ka, kb, k0], 3: [ka, kb, kc, k0]}
    v_sets = {0: [v0], 1: [vc, v0], 2: [va, vb, v0], 3: [va, vb, vc, v0]}
    for d in range(4):
        @pl.when(me == d)
        def _():
            attn_one(head_dim, n_kv, chunk, q_ref, k_sets[d], v_sets[d], o_ref)


def attention(me, q, kvs, head_dim, n_kv, chunk=2):
    n_batch, feats, s = q.shape
    kv = n_kv * head_dim
    flat = [a for pair in kvs for a in pair]
    kspec = pl.BlockSpec((1, s, kv), lambda b, me_ref: (b, 0, 0))
    vspec = pl.BlockSpec((1, kv, s), lambda b, me_ref: (b, 0, 0))
    return pl.pallas_call(
        functools.partial(attn_body, head_dim, n_kv, chunk),
        grid_spec=pltpu.PrefetchScalarGridSpec(
            num_scalar_prefetch=1,
            grid=(n_batch,),
            in_specs=[pl.BlockSpec((1, feats, s), lambda b, me_ref: (b, 0, 0))] + [kspec, vspec] * 4,
            out_specs=pl.BlockSpec((1, s, feats), lambda b, me_ref: (b, 0, 0)),
        ),
        out_shape=jax.ShapeDtypeStruct((n_batch, s, feats), BF16),
        compiler_params=params(),
        cost_estimate=cost(4 * n_batch * feats * s * 256, 4 * n_batch * feats * s),
        name="attention",
    )(me, q, *flat)


def out_body(o_ref, w_ref, x_ref, g_ref, h_ref, r_ref):
    acc = jnp.dot(o_ref[...], w_ref[0], preferred_element_type=F32)
    h = (x_ref[...].astype(F32) + acc).astype(BF16)
    h_ref[...] = h
    r_ref[...] = normed(h, g_ref[0])


def out_proj(layer, o, w, x, gain, tile=256):
    rows, d = x.shape
    k = o.shape[1]
    return pl.pallas_call(
        out_body,
        grid=(rows // tile,),
        in_specs=[
            pl.BlockSpec((tile, k), lambda i: (i, 0)),
            pl.BlockSpec((1, k, d), lambda i: (layer, 0, 0), pipeline_mode=pl.Buffered(1)),
            pl.BlockSpec((tile, d), lambda i: (i, 0)),
            pl.BlockSpec((1, 1, d), lambda i: (layer, 0, 0)),
        ],
        out_specs=[pl.BlockSpec((tile, d), lambda i: (i, 0))] * 2,
        out_shape=[jax.ShapeDtypeStruct((rows, d), BF16)] * 2,
        compiler_params=params(),
        cost_estimate=cost(2 * rows * d * k, 8 * rows * d),
        name="out_proj",
    )(o, w, x, gain)


def mlp_body(n_up, tn, mt, r_ref, wu_ref, wd_ref, h_ref, y_ref, z_ref):
    i = pl.program_id(0)
    rows = r_ref.shape[0]

    @pl.when(i < n_up)
    def _():
        cols = pl.ds(pl.multiple_of(i * tn, tn), tn)
        for m in range(0, rows, mt):
            u = jnp.dot(r_ref[m:m + mt, :], wu_ref[0], preferred_element_type=F32)
            z_ref[m:m + mt, cols] = jax.nn.gelu(u, approximate=True).astype(BF16)

    @pl.when(i >= n_up)
    def _():
        for m in range(0, rows, mt):
            acc = jnp.dot(z_ref[m:m + mt, :], wd_ref[0], preferred_element_type=F32)
            y_ref[m:m + mt, :] = (h_ref[m:m + mt, :].astype(F32) + acc).astype(BF16)


def mlp(layer, r, wu, wd, h, tn=512, td=512, mt=1024):
    rows, d = r.shape
    ff = wu.shape[2]
    n_up = ff // tn
    n_dn = d // td
    return pl.pallas_call(
        functools.partial(mlp_body, n_up, tn, mt),
        grid=(n_up + n_dn,),
        in_specs=[
            pl.BlockSpec((rows, d), lambda i: (0, 0), pipeline_mode=pl.Buffered(1)),
            pl.BlockSpec((1, d, tn), lambda i: (layer, 0, jnp.minimum(i, n_up - 1))),
            pl.BlockSpec((1, ff, td), lambda i: (layer, 0, jnp.maximum(i - n_up, 0))),
            pl.BlockSpec((rows, td), lambda i: (0, jnp.maximum(i - n_up, 0))),
        ],
        out_specs=pl.BlockSpec((rows, td), lambda i: (0, jnp.maximum(i - n_up, 0))),
        out_shape=jax.ShapeDtypeStruct((rows, d), BF16),
        scratch_shapes=[pltpu.VMEM((rows, ff), BF16)],
        compiler_params=params(),
        cost_estimate=cost(4 * rows * d * ff, 4 * ff * d),
        name="mlp",
    )(r, wu, wd, h)


def solution(mesh):
    tok_spec = P(None, ("data", "seq"), None)
    in_specs = (tok_spec, P(("data", "seq"))) + (P(),) * 8

    def device_fn(x_loc, pos_loc, w_query, w_key, w_value, w_out, w_up, w_down, g_attn, g_mlp):
        n_layers, d, n_heads, head_dim = w_query.shape
        n_kv = w_key.shape[2]
        n_batch, s, _ = x_loc.shape
        rows = n_batch * s
        half = head_dim // 2
        inv_freq = ROPE_BASE ** (-jnp.arange(half, dtype=F32) * (2.0 / head_dim))
        angles = inv_freq[:, None] * pos_loc.astype(F32)[None, :]
        cos, sin = jnp.cos(angles), jnp.sin(angles)
        wq = jnp.transpose(w_query, (0, 2, 3, 1)).reshape(n_layers, n_heads * head_dim, d)
        wk = jnp.transpose(w_key, (0, 2, 3, 1)).reshape(n_layers, n_kv * head_dim, d)
        wv = jnp.transpose(w_value, (0, 2, 3, 1)).reshape(n_layers, n_kv * head_dim, d)
        wo = w_out.reshape(n_layers, n_heads * head_dim, d)
        ga = g_attn.reshape(n_layers, 1, d)
        gm = g_mlp.reshape(n_layers, 1, d)
        me = lax.axis_index("seq").astype(jnp.int32).reshape(1)
        x = x_loc.reshape(rows, d)
        for layer in range(n_layers):
            n, k, v = kv_proj(layer, x, ga, wk, wv, cos, sin, head_dim, n_batch)
            cross = [lax.ppermute(a, "seq", ((0, 2), (1, 3))) for a in (k, v)]
            near = [lax.ppermute(a, "seq", ((0, 1), (2, 3))) for a in (k, v)]
            q = q_proj(layer, n, wq, cos, sin, head_dim, n_batch)
            swap = [lax.ppermute(a, "seq", ((2, 3), (3, 2))) for a in cross]
            o = attention(me, q, ((k, v), cross, swap, near), head_dim, n_kv)
            h, r = out_proj(layer, o.reshape(rows, n_heads * head_dim), wo, x, gm)
            x = mlp(layer, r, w_up, w_down, h)
        return x.reshape(x_loc.shape)

    return jax.shard_map(device_fn, mesh=mesh, in_specs=in_specs, out_specs=tok_spec, check_vma=False)
```

time: 2100 us -> 988 us (0.47)
  matrix products: 867 us -> 0 us
  Pallas kernels: 0 us -> 857 us
  local copies, waits for them, and re-layouts: 394 us -> 2.75 us
  waiting for transfers between devices: 373 us -> 91.1 us
  blocking collectives: 201 us -> 0 us
  other arithmetic: 195 us -> 1.42 us
  starting transfers between devices: 54.5 us -> 30.9 us
    dot_general x30 -> x0, matrix products: 867 us -> none  [the longest x3 188 us: layer_step(): jnp.einsum('bsd,df->bsf', normed_mlp, w_up, preferred_element_type=jnp.fl...]
    pallas_call x0 -> x15, Pallas kernels: none -> 857 us  [the longest x3 343 us: mlp(): pl.pallas_call(functools.partial(mlp_body, n_up, tn, mt), grid=(n_up + n_...]
    all_to_all x10 -> x0, waiting for transfers between devices: 373 us -> none  [the longest x3 271 us: layer_step(): q_all = lax.all_to_all(q_loc, 'seq', 2, 1, tiled=True)]
    all_to_all x2 -> x0, blocking collectives: 201 us -> none  [layer_step(): attn_loc = lax.all_to_all(attn_heads, 'seq', 1, 2, tiled=True)]
    reduce_sum x7 -> x0, other arithmetic: 134 us -> none  [the longest x6 129 us: one_block(): row_sum = jnp.sum(exp_f32, axis=-1)]
    all_to_all x15 -> x0, local copies, waits for them, and re-layouts: 120 us -> none  [the longest x6 85 us: layer_step(): attn_loc = lax.all_to_all(attn_heads, 'seq', 1, 2, tiled=True)]
    reshape x6 -> x2, local copies, waits for them, and re-layouts: 121 us -> 2.75 us  [the longest x1 1.38 us: device_fn(): gm = g_mlp.reshape(n_layers, 1, d)]
    unnamed x34 -> x0, local copies, waits for them, and re-layouts: 97.6 us -> none
  transfers between devices with their start and end apart: 10 -> 18, of which waited for: 6 -> 6; matrix products, arithmetic and copies ran while one was open for 6% -> 0% of each run, Pallas kernels for 0% -> 7%
where the time goes in v1:
time: 988 us; the launch traced here: 984 us
  Pallas kernels  857 us (87%)
  waiting for transfers between devices  91.1 us (9%)
  starting transfers between devices  30.9 us (3%)
    pallas_call x3, Pallas kernels, mlp(): pl.pallas_call(functools.partial(mlp_body, n_up, tn, mt), grid=(n_up + n_...  343 us
    pallas_call x3, Pallas kernels, attention(): pl.pallas_call(functools.partial(attn_body, head_dim, n_kv, chunk), grid_...  324 us
    ppermute x6, waiting for transfers between devices, device_fn(): cross = [lax.ppermute(a, 'seq', ((0, 2), (1, 3))) for a in (k, v)]  91.1 us
    pallas_call x3, Pallas kernels, out_proj(): pl.pallas_call(out_body, grid=(rows // tile,), in_specs=[pl.BlockSpec((ti...  80.3 us
    pallas_call x3, Pallas kernels, q_proj(): pl.pallas_call(functools.partial(q_body, head_dim, s, fchunk), grid=(rows...  72.5 us
    pallas_call x3, Pallas kernels, kv_proj(): pl.pallas_call(functools.partial(kv_body, head_dim, s), grid=(rows // til...  36.5 us
  transfers between devices with their start and end apart: 18, of which 6 were waited for; matrix products, arithmetic and copies ran while one was open for 0% of the time, Pallas kernels for 7%

profile of v1, /device:TPU:7, one launch (start us, length us, event | category | flops | bytes accessed | tf_op | source)
XLA Modules:
  0.0 983.7 jit_solution(17611666631865118050)
XLA Ops:
  2.8 12.2 %kv_proj.3 = (bf16[2048,2048]{1,0:T(8,128)(2,1)}, bf16[16,128,256]{2,1,0:T(8,128)(2,1)}, bf16[16,256,128]{2,1,0:T(8,128)(2,1)}) custom-call(bf16[2048,2048]{1,0:T(8,128)(2,1)} %bitcast.25, f32[3,1,2048]{2,1,0:T(1,128)} %reshape.45.g_ref, bf16[3,256,2048]{2,1,0:T(8,128)(2,1)} %bitcast.27, bf16[3,256,2048]{2,1,0:T(8,128)(2,1)} %bitcast.30, ...), custom_call_target="tpu_custom_call" | custom-call | flops 4294967296 | bytes 16777216 | tf_op jit(solution)/shard_map/kv_proj/pallas_call | solution.py:56
  21.5 19.5 %collective-permute-done.ka = bf16[16,128,256]{2,1,0:T(8,128)(2,1)} collective-permute-done((bf16[16,128,256]{2,1,0:T(8,128)(2,1)}, bf16[16,128,256]{2,1,0:T(8,128)(2,1)}, u32[]{:S(2)}, u32[]{:S(2)}) %collective-permute-start) | collective-permute-done | bytes 1048608 | tf_op jit(solution)/shard_map/ppermute | solution.py:271
  41.0 4.5 collective-permute-start.2
  45.5 18.0 %collective-permute-done.1.va = bf16[16,256,128]{2,1,0:T(8,128)(2,1)} collective-permute-done((bf16[16,256,128]{2,1,0:T(8,128)(2,1)}, bf16[16,256,128]{2,1,0:T(8,128)(2,1)}, u32[]{:S(2)}, u32[]{:S(2)}) %collective-permute-start.1) | collective-permute-done | bytes 1048608 | tf_op jit(solution)/shard_map/ppermute | solution.py:271
  63.5 3.3 collective-permute-start.3
  66.8 24.2 %q_proj.3.q_ref = bf16[16,2048,128]{2,1,0:T(8,128)(2,1)} custom-call(bf16[2048,2048]{1,0:T(8,128)(2,1)} %get-tuple-element.20.n_ref, bf16[3,2048,2048]{2,1,0:T(8,128)(2,1)} %bitcast.19, f32[32,128]{1,0:T(8,128)} %get-tuple-element.36.cos_ref, f32[32,128]{1,0:T(8,128)} %get-tuple-element.35.sin_ref), custom_call_target="tpu_custom_call" | custom-call | flops 17179869184 | bytes 25165824 | tf_op jit(solution)/shard_map/q_proj/pallas_call | solution.py:98
  91.1 108.1 %attention.3 = bf16[16,128,2048]{2,1,0:T(8,128)(2,1)} custom-call(s32[1]{0:T(128)} %bitcast.me_ref, bf16[16,2048,128]{2,1,0:T(8,128)(2,1)} %q_proj.3.q_ref, bf16[16,128,256]{2,1,0:T(8,128)(2,1)} %get-tuple-element.21.k0, bf16[16,256,128]{2,1,0:T(8,128)(2,1)} %get-tuple-element.22.v0, bf16[16,128,256]{2,1,0:T(8,128)(2,1)} %collective-permute-done.ka, ...), custom_call_target="tpu_custom_call" | custom-call | flops 4294967296 | bytes 16777216 | tf_op jit(solution)/shard_map/attention/pallas_call | solution.py:165
  199.2 26.6 %out_proj.3 = (bf16[2048,2048]{1,0:T(8,128)(2,1)}, bf16[2048,2048]{1,0:T(8,128)(2,1)}) custom-call(bf16[2048,2048]{1,0:T(8,128)(2,1)} %bitcast.18, bf16[3,2048,2048]{2,1,0:T(8,128)(2,1)} %bitcast.22, bf16[2048,2048]{1,0:T(8,128)(2,1)} %bitcast.26, f32[3,1,2048]{2,1,0:T(1,128)} %reshape.51.g_ref), custom_call_target="tpu_custom_call" | custom-call | flops 17179869184 | bytes 33554432 | tf_op jit(solution)/shard_map/out_proj/pallas_call | solution.py:190
  225.9 114.5 %mlp.3.x_ref = bf16[2048,2048]{1,0:T(8,128)(2,1)} custom-call(bf16[2048,2048]{1,0:T(8,128)(2,1)} %get-tuple-element.23.r_ref, bf16[3,2048,5632]{2,1,0:T(8,128)(2,1)} %wu_ref.5, bf16[3,5632,2048]{2,1,0:T(8,128)(2,1)} %wd_ref.5, bf16[2048,2048]{1,0:T(8,128)(2,1)} %get-tuple-element.24.h_ref), custom_call_target="tpu_custom_call" | custom-call | flops 94489280512 | bytes 46137344 | tf_op jit(solution)/shard_map/mlp/pallas_call | solution.py:230
  340.3 12.2 %kv_proj.4 = (bf16[2048,2048]{1,0:T(8,128)(2,1)}, bf16[16,128,256]{2,1,0:T(8,128)(2,1)}, bf16[16,256,128]{2,1,0:T(8,128)(2,1)}) custom-call(bf16[2048,2048]{1,0:T(8,128)(2,1)} %mlp.3.x_ref, f32[3,1,2048]{2,1,0:T(1,128)} %reshape.45.g_ref, bf16[3,256,2048]{2,1,0:T(8,128)(2,1)} %bitcast.28, bf16[3,256,2048]{2,1,0:T(8,128)(2,1)} %bitcast.31, ...), custom_call_target="tpu_custom_call" | custom-call | flops 4294967296 | bytes 16777216 | tf_op jit(solution)/shard_map/kv_proj/pallas_call | solution.py:56
  357.7 17.3 %collective-permute-done.6.ka = bf16[16,128,256]{2,1,0:T(8,128)(2,1)} collective-permute-done((bf16[16,128,256]{2,1,0:T(8,128)(2,1)}, bf16[16,128,256]{2,1,0:T(8,128)(2,1)}, u32[]{:S(2)}, u32[]{:S(2)}) %collective-permute-start.6) | collective-permute-done | bytes 1048608 | tf_op jit(solution)/shard_map/ppermute | solution.py:271
  374.9 1.9 collective-permute-start.8
  376.9 9.3 collective-permute-done.7.va
  388.1 24.1 %q_proj.4.q_ref = bf16[16,2048,128]{2,1,0:T(8,128)(2,1)} custom-call(bf16[2048,2048]{1,0:T(8,128)(2,1)} %get-tuple-element.25.n_ref, bf16[3,2048,2048]{2,1,0:T(8,128)(2,1)} %bitcast.20, f32[32,128]{1,0:T(8,128)} %get-tuple-element.36.cos_ref, f32[32,128]{1,0:T(8,128)} %get-tuple-element.35.sin_ref), custom_call_target="tpu_custom_call" | custom-call | flops 17179869184 | bytes 25165824 | tf_op jit(solution)/shard_map/q_proj/pallas_call | solution.py:98
  412.2 108.2 %attention.4 = bf16[16,128,2048]{2,1,0:T(8,128)(2,1)} custom-call(s32[1]{0:T(128)} %bitcast.me_ref, bf16[16,2048,128]{2,1,0:T(8,128)(2,1)} %q_proj.4.q_ref, bf16[16,128,256]{2,1,0:T(8,128)(2,1)} %get-tuple-element.26.k0, bf16[16,256,128]{2,1,0:T(8,128)(2,1)} %get-tuple-element.27.v0, bf16[16,128,256]{2,1,0:T(8,128)(2,1)} %collective-permute-done.6.ka, ...), custom_call_target="tpu_custom_call" | custom-call | flops 4294967296 | bytes 16777216 | tf_op jit(solution)/shard_map/attention/pallas_call | solution.py:165
  520.4 26.7 %out_proj.4 = (bf16[2048,2048]{1,0:T(8,128)(2,1)}, bf16[2048,2048]{1,0:T(8,128)(2,1)}) custom-call(bf16[2048,2048]{1,0:T(8,128)(2,1)} %bitcast.17, bf16[3,2048,2048]{2,1,0:T(8,128)(2,1)} %bitcast.23, bf16[2048,2048]{1,0:T(8,128)(2,1)} %mlp.3.x_ref, f32[3,1,2048]{2,1,0:T(1,128)} %reshape.51.g_ref), custom_call_target="tpu_custom_call" | custom-call | flops 17179869184 | bytes 33554432 | tf_op jit(solution)/shard_map/out_proj/pallas_call | solution.py:190
  547.2 114.5 %mlp.4.x_ref = bf16[2048,2048]{1,0:T(8,128)(2,1)} custom-call(bf16[2048,2048]{1,0:T(8,128)(2,1)} %get-tuple-element.28.r_ref, bf16[3,2048,5632]{2,1,0:T(8,128)(2,1)} %wu_ref.5, bf16[3,5632,2048]{2,1,0:T(8,128)(2,1)} %wd_ref.5, bf16[2048,2048]{1,0:T(8,128)(2,1)} %get-tuple-element.29.h_ref), custom_call_target="tpu_custom_call" | custom-call | flops 94489280512 | bytes 46137344 | tf_op jit(solution)/shard_map/mlp/pallas_call | solution.py:230
  661.7 12.2 %kv_proj.5 = (bf16[2048,2048]{1,0:T(8,128)(2,1)}, bf16[16,128,256]{2,1,0:T(8,128)(2,1)}, bf16[16,256,128]{2,1,0:T(8,128)(2,1)}) custom-call(bf16[2048,2048]{1,0:T(8,128)(2,1)} %mlp.4.x_ref, f32[3,1,2048]{2,1,0:T(1,128)} %reshape.45.g_ref, bf16[3,256,2048]{2,1,0:T(8,128)(2,1)} %bitcast.29, bf16[3,256,2048]{2,1,0:T(8,128)(2,1)} %bitcast.32, ...), custom_call_target="tpu_custom_call" | custom-call | flops 4294967296 | bytes 16777216 | tf_op jit(solution)/shard_map/kv_proj/pallas_call | solution.py:56
  679.0 17.7 %collective-permute-done.12.ka = bf16[16,128,256]{2,1,0:T(8,128)(2,1)} collective-permute-done((bf16[16,128,256]{2,1,0:T(8,128)(2,1)}, bf16[16,128,256]{2,1,0:T(8,128)(2,1)}, u32[]{:S(2)}, u32[]{:S(2)}) %collective-permute-start.12) | collective-permute-done | bytes 1048608 | tf_op jit(solution)/shard_map/ppermute | solution.py:271
  698.7 9.3 collective-permute-done.13.va
  709.9 24.2 %q_proj.5.q_ref = bf16[16,2048,128]{2,1,0:T(8,128)(2,1)} custom-call(bf16[2048,2048]{1,0:T(8,128)(2,1)} %get-tuple-element.30.n_ref, bf16[3,2048,2048]{2,1,0:T(8,128)(2,1)} %bitcast.21, f32[32,128]{1,0:T(8,128)} %get-tuple-element.36.cos_ref, f32[32,128]{1,0:T(8,128)} %get-tuple-element.35.sin_ref), custom_call_target="tpu_custom_call" | custom-call | flops 17179869184 | bytes 25165824 | tf_op jit(solution)/shard_map/q_proj/pallas_call | solution.py:98
  734.1 107.9 %attention.5 = bf16[16,128,2048]{2,1,0:T(8,128)(2,1)} custom-call(s32[1]{0:T(128)} %bitcast.me_ref, bf16[16,2048,128]{2,1,0:T(8,128)(2,1)} %q_proj.5.q_ref, bf16[16,128,256]{2,1,0:T(8,128)(2,1)} %get-tuple-element.31.k0, bf16[16,256,128]{2,1,0:T(8,128)(2,1)} %get-tuple-element.32.v0, bf16[16,128,256]{2,1,0:T(8,128)(2,1)} %collective-permute-done.12.ka, ...), custom_call_target="tpu_custom_call" | custom-call | flops 4294967296 | bytes 16777216 | tf_op jit(solution)/shard_map/attention/pallas_call | solution.py:165
  842.1 26.9 %out_proj.5 = (bf16[2048,2048]{1,0:T(8,128)(2,1)}, bf16[2048,2048]{1,0:T(8,128)(2,1)}) custom-call(bf16[2048,2048]{1,0:T(8,128)(2,1)} %bitcast.16, bf16[3,2048,2048]{2,1,0:T(8,128)(2,1)} %bitcast.24, bf16[2048,2048]{1,0:T(8,128)(2,1)} %mlp.4.x_ref, f32[3,1,2048]{2,1,0:T(1,128)} %reshape.51.g_ref), custom_call_target="tpu_custom_call" | custom-call | flops 17179869184 | bytes 33554432 | tf_op jit(solution)/shard_map/out_proj/pallas_call | solution.py:190
  869.0 114.5 %mlp.5 = bf16[2048,2048]{1,0:T(8,128)(2,1)} custom-call(bf16[2048,2048]{1,0:T(8,128)(2,1)} %get-tuple-element.33.r_ref, bf16[3,2048,5632]{2,1,0:T(8,128)(2,1)} %wu_ref.5, bf16[3,5632,2048]{2,1,0:T(8,128)(2,1)} %wd_ref.5, bf16[2048,2048]{1,0:T(8,128)(2,1)} %get-tuple-element.34.h_ref), custom_call_target="tpu_custom_call" | custom-call | flops 94489280512 | bytes 46137344 | tf_op jit(solution)/shard_map/mlp/pallas_call | solution.py:230
  (32 shorter events, 25.4 us)
Async XLA Ops:
  15.0 26.0 %collective-permute-start = (bf16[16,128,256]{2,1,0:T(8,128)(2,1)}, bf16[16,128,256]{2,1,0:T(8,128)(2,1)}, u32[]{:S(2)}, u32[]{:S(2)}) collective-permute-start(bf16[16,128,256]{2,1,0:T(8,128)(2,1)} %get-tuple-element.21.k0), channel_id=1, source_target_pairs={{0,2},{1,3},{4,6},{5,7},{8,10},{9,11},{12,14},{13,15}} | collective-permute-start | bytes 3145736 | tf_op jit(solution)/shard_map/ppermute | solution.py:271
  16.2 47.2 %collective-permute-start.1 = (bf16[16,256,128]{2,1,0:T(8,128)(2,1)}, bf16[16,256,128]{2,1,0:T(8,128)(2,1)}, u32[]{:S(2)}, u32[]{:S(2)}) collective-permute-start(bf16[16,256,128]{2,1,0:T(8,128)(2,1)} %get-tuple-element.22.v0), channel_id=1, source_target_pairs={{0,2},{1,3},{4,6},{5,7},{8,10},{9,11},{12,14},{13,15}} | collective-permute-start | bytes 3145736 | tf_op jit(solution)/shard_map/ppermute | solution.py:271
  17.5 73.5 %collective-permute-start.4 = (bf16[16,128,256]{2,1,0:T(8,128)(2,1)}, bf16[16,128,256]{2,1,0:T(8,128)(2,1)}, u32[]{:S(2)}, u32[]{:S(2)}) collective-permute-start(bf16[16,128,256]{2,1,0:T(8,128)(2,1)} %get-tuple-element.21.k0), channel_id=1, source_target_pairs={{0,1},{2,3},{4,5},{6,7},{8,9},{10,11},{12,13},{14,15}} | collective-permute-start | bytes 3145736 | tf_op jit(solution)/shard_map/ppermute | solution.py:272
  18.8 72.2 %collective-permute-start.5 = (bf16[16,256,128]{2,1,0:T(8,128)(2,1)}, bf16[16,256,128]{2,1,0:T(8,128)(2,1)}, u32[]{:S(2)}, u32[]{:S(2)}) collective-permute-start(bf16[16,256,128]{2,1,0:T(8,128)(2,1)} %get-tuple-element.22.v0), channel_id=1, source_target_pairs={{0,1},{2,3},{4,5},{6,7},{8,9},{10,11},{12,13},{14,15}} | collective-permute-start | bytes 3145736 | tf_op jit(solution)/shard_map/ppermute | solution.py:272
  41.0 50.0 %collective-permute-start.2 = (bf16[16,128,256]{2,1,0:T(8,128)(2,1)}, bf16[16,128,256]{2,1,0:T(8,128)(2,1)}, u32[]{:S(2)}, u32[]{:S(2)}) collective-permute-start(bf16[16,128,256]{2,1,0:T(8,128)(2,1)} %collective-permute-done.ka), channel_id=1, source_target_pairs={{2,3},{3,2},{6,7},{7,6},{10,11},{11,10},{14,15},{15,14}} | collective-permute-start | bytes 3145736 | tf_op jit(solution)/shard_map/ppermute | solution.py:274
  63.5 27.6 %collective-permute-start.3 = (bf16[16,256,128]{2,1,0:T(8,128)(2,1)}, bf16[16,256,128]{2,1,0:T(8,128)(2,1)}, u32[]{:S(2)}, u32[]{:S(2)}) collective-permute-start(bf16[16,256,128]{2,1,0:T(8,128)(2,1)} %collective-permute-done.1.va), channel_id=1, source_target_pairs={{2,3},{3,2},{6,7},{7,6},{10,11},{11,10},{14,15},{15,14}} | collective-permute-start | bytes 3145736 | tf_op jit(solution)/shard_map/ppermute | solution.py:274
  352.5 22.4 %collective-permute-start.6 = (bf16[16,128,256]{2,1,0:T(8,128)(2,1)}, bf16[16,128,256]{2,1,0:T(8,128)(2,1)}, u32[]{:S(2)}, u32[]{:S(2)}) collective-permute-start(bf16[16,128,256]{2,1,0:T(8,128)(2,1)} %get-tuple-element.26.k0), channel_id=1, source_target_pairs={{0,2},{1,3},{4,6},{5,7},{8,10},{9,11},{12,14},{13,15}} | collective-permute-start | bytes 3145736 | tf_op jit(solution)/shard_map/ppermute | solution.py:271
  353.8 32.4 %collective-permute-start.7 = (bf16[16,256,128]{2,1,0:T(8,128)(2,1)}, bf16[16,256,128]{2,1,0:T(8,128)(2,1)}, u32[]{:S(2)}, u32[]{:S(2)}) collective-permute-start(bf16[16,256,128]{2,1,0:T(8,128)(2,1)} %get-tuple-element.27.v0), channel_id=1, source_target_pairs={{0,2},{1,3},{4,6},{5,7},{8,10},{9,11},{12,14},{13,15}} | collective-permute-start | bytes 3145736 | tf_op jit(solution)/shard_map/ppermute | solution.py:271
  355.1 57.1 %collective-permute-start.10 = (bf16[16,128,256]{2,1,0:T(8,128)(2,1)}, bf16[16,128,256]{2,1,0:T(8,128)(2,1)}, u32[]{:S(2)}, u32[]{:S(2)}) collective-permute-start(bf16[16,128,256]{2,1,0:T(8,128)(2,1)} %get-tuple-element.26.k0), channel_id=1, source_target_pairs={{0,1},{2,3},{4,5},{6,7},{8,9},{10,11},{12,13},{14,15}} | collective-permute-start | bytes 3145736 | tf_op jit(solution)/shard_map/ppermute | solution.py:272
  356.4 55.8 %collective-permute-start.11 = (bf16[16,256,128]{2,1,0:T(8,128)(2,1)}, bf16[16,256,128]{2,1,0:T(8,128)(2,1)}, u32[]{:S(2)}, u32[]{:S(2)}) collective-permute-start(bf16[16,256,128]{2,1,0:T(8,128)(2,1)} %get-tuple-element.27.v0), channel_id=1, source_target_pairs={{0,1},{2,3},{4,5},{6,7},{8,9},{10,11},{12,13},{14,15}} | collective-permute-start | bytes 3145736 | tf_op jit(solution)/shard_map/ppermute | solution.py:272
  374.9 37.3 %collective-permute-start.8 = (bf16[16,128,256]{2,1,0:T(8,128)(2,1)}, bf16[16,128,256]{2,1,0:T(8,128)(2,1)}, u32[]{:S(2)}, u32[]{:S(2)}) collective-permute-start(bf16[16,128,256]{2,1,0:T(8,128)(2,1)} %collective-permute-done.6.ka), channel_id=1, source_target_pairs={{2,3},{3,2},{6,7},{7,6},{10,11},{11,10},{14,15},{15,14}} | collective-permute-start | bytes 3145736 | tf_op jit(solution)/shard_map/ppermute | solution.py:274
  386.2 26.1 %collective-permute-start.9 = (bf16[16,256,128]{2,1,0:T(8,128)(2,1)}, bf16[16,256,128]{2,1,0:T(8,128)(2,1)}, u32[]{:S(2)}, u32[]{:S(2)}) collective-permute-start(bf16[16,256,128]{2,1,0:T(8,128)(2,1)} %collective-permute-done.7.va), channel_id=1, source_target_pairs={{2,3},{3,2},{6,7},{7,6},{10,11},{11,10},{14,15},{15,14}} | collective-permute-start | bytes 3145736 | tf_op jit(solution)/shard_map/ppermute | solution.py:274
  673.8 22.9 %collective-permute-start.12 = (bf16[16,128,256]{2,1,0:T(8,128)(2,1)}, bf16[16,128,256]{2,1,0:T(8,128)(2,1)}, u32[]{:S(2)}, u32[]{:S(2)}) collective-permute-start(bf16[16,128,256]{2,1,0:T(8,128)(2,1)} %get-tuple-element.31.k0), channel_id=1, source_target_pairs={{0,2},{1,3},{4,6},{5,7},{8,10},{9,11},{12,14},{13,15}} | collective-permute-start | bytes 3145736 | tf_op jit(solution)/shard_map/ppermute | solution.py:271
  675.1 32.9 %collective-permute-start.13 = (bf16[16,256,128]{2,1,0:T(8,128)(2,1)}, bf16[16,256,128]{2,1,0:T(8,128)(2,1)}, u32[]{:S(2)}, u32[]{:S(2)}) collective-permute-start(bf16[16,256,128]{2,1,0:T(8,128)(2,1)} %get-tuple-element.32.v0), channel_id=1, source_target_pairs={{0,2},{1,3},{4,6},{5,7},{8,10},{9,11},{12,14},{13,15}} | collective-permute-start | bytes 3145736 | tf_op jit(solution)/shard_map/ppermute | solution.py:271
  676.4 57.6 %collective-permute-start.16 = (bf16[16,128,256]{2,1,0:T(8,128)(2,1)}, bf16[16,128,256]{2,1,0:T(8,128)(2,1)}, u32[]{:S(2)}, u32[]{:S(2)}) collective-permute-start(bf16[16,128,256]{2,1,0:T(8,128)(2,1)} %get-tuple-element.31.k0), channel_id=1, source_target_pairs={{0,1},{2,3},{4,5},{6,7},{8,9},{10,11},{12,13},{14,15}} | collective-permute-start | bytes 3145736 | tf_op jit(solution)/shard_map/ppermute | solution.py:272
  677.7 56.4 %collective-permute-start.17 = (bf16[16,256,128]{2,1,0:T(8,128)(2,1)}, bf16[16,256,128]{2,1,0:T(8,128)(2,1)}, u32[]{:S(2)}, u32[]{:S(2)}) collective-permute-start(bf16[16,256,128]{2,1,0:T(8,128)(2,1)} %get-tuple-element.32.v0), channel_id=1, source_target_pairs={{0,1},{2,3},{4,5},{6,7},{8,9},{10,11},{12,13},{14,15}} | collective-permute-start | bytes 3145736 | tf_op jit(solution)/shard_map/ppermute | solution.py:272
  696.7 37.3 %collective-permute-start.14 = (bf16[16,128,256]{2,1,0:T(8,128)(2,1)}, bf16[16,128,256]{2,1,0:T(8,128)(2,1)}, u32[]{:S(2)}, u32[]{:S(2)}) collective-permute-start(bf16[16,128,256]{2,1,0:T(8,128)(2,1)} %collective-permute-done.12.ka), channel_id=1, source_target_pairs={{2,3},{3,2},{6,7},{7,6},{10,11},{11,10},{14,15},{15,14}} | collective-permute-start | bytes 3145736 | tf_op jit(solution)/shard_map/ppermute | solution.py:274
  708.0 26.1 %collective-permute-start.15 = (bf16[16,256,128]{2,1,0:T(8,128)(2,1)}, bf16[16,256,128]{2,1,0:T(8,128)(2,1)}, u32[]{:S(2)}, u32[]{:S(2)}) collective-permute-start(bf16[16,256,128]{2,1,0:T(8,128)(2,1)} %collective-permute-done.13.va), channel_id=1, source_target_pairs={{2,3},{3,2},{6,7},{7,6},{10,11},{11,10},{14,15},{15,14}} | collective-permute-start | bytes 3145736 | tf_op jit(solution)/shard_map/ppermute | solution.py:274

commit v2 on v1

v2 whole, which is shorter than its diff:
```python
import functools

import jax
import jax.numpy as jnp
from jax import lax
from jax.experimental import pallas as pl
from jax.experimental.pallas import tpu as pltpu
from jax.sharding import PartitionSpec as P

ROPE_BASE = 10000.0
NORM_EPS = 1e-6
LOG2E = 1.4426950408889634
F32 = jnp.float32
BF16 = jnp.bfloat16
LANES = 128
NT = (((1,), (1,)), ((), ()))
VMEM_LIMIT = 64 * 1024 * 1024 - 65536


def params(limit=VMEM_LIMIT):
    return pltpu.CompilerParams(dimension_semantics=("arbitrary",), vmem_limit_bytes=limit)


def cost(flops, nbytes):
    return pl.CostEstimate(flops=int(flops), bytes_accessed=int(nbytes), transcendentals=0)


def normed(x_bf16, gain):
    x = x_bf16.astype(F32)
    mean_sq = jnp.mean(x * x, axis=-1, keepdims=True)
    return (x * lax.rsqrt(mean_sq + NORM_EPS) * gain).astype(BF16)


def rope_t(u, cos, sin):
    half = u.shape[0] // 2
    a, b = u[:half], u[half:]
    return jnp.concatenate([a * cos - b * sin, b * cos + a * sin], axis=0).astype(BF16)


def kv_body(head_dim, batch_rows, x_ref, g_ref, wk_ref, wv_ref, cos_ref, sin_ref, n_ref, kv_ref):
    n = normed(x_ref[...], g_ref[0])
    n_ref[...] = n
    k_t = lax.dot_general(wk_ref[0], n, NT, preferred_element_type=F32)
    v_t = lax.dot_general(wv_ref[0], n, NT, preferred_element_type=F32).astype(BF16)
    kv = k_t.shape[0]
    for i in range(n.shape[0] // batch_rows):
        cols = slice(i * batch_rows, (i + 1) * batch_rows)
        heads = [rope_t(k_t[h:h + head_dim, cols], cos_ref[...], sin_ref[...]) for h in range(0, kv, head_dim)]
        per = LANES // head_dim
        for p in range(kv // LANES):
            pair = jnp.concatenate(heads[p * per:(p + 1) * per], axis=0)
            kv_ref[i, p * batch_rows:(p + 1) * batch_rows, :] = pair.T
        kv_ref[i, kv // LANES * batch_rows:, :] = v_t[:, cols]


def kv_proj(layer, x, gain, wk, wv, cos, sin, head_dim, n_batch, tile=256):
    rows, d = x.shape
    kv = wk.shape[1]
    s = rows // n_batch
    per = tile // s
    kv_rows = kv // LANES * s + kv
    return pl.pallas_call(
        functools.partial(kv_body, head_dim, s),
        grid=(rows // tile,),
        in_specs=[
            pl.BlockSpec((tile, d), lambda i: (i, 0)),
            pl.BlockSpec((1, 1, d), lambda i: (layer, 0, 0)),
            pl.BlockSpec((1, kv, d), lambda i: (layer, 0, 0)),
            pl.BlockSpec((1, kv, d), lambda i: (layer, 0, 0)),
            pl.BlockSpec(cos.shape, lambda i: (0, 0)),
            pl.BlockSpec(cos.shape, lambda i: (0, 0)),
        ],
        out_specs=[
            pl.BlockSpec((tile, d), lambda i: (i, 0)),
            pl.BlockSpec((per, kv_rows, s), lambda i: (i, 0, 0)),
        ],
        out_shape=[
            jax.ShapeDtypeStruct((rows, d), BF16),
            jax.ShapeDtypeStruct((n_batch, kv_rows, s), BF16),
        ],
        compiler_params=params(),
        cost_estimate=cost(4 * rows * d * kv, 4 * rows * d),
        name="kv_proj",
    )(x, gain, wk, wv, cos, sin)


def attn_one(head_dim, n_kv, q_ref, b, refs, o_ref):
    s = q_ref.shape[2]
    groups = q_ref.shape[1] // head_dim // n_kv
    factor = LOG2E * head_dim ** -0.5
    pack = LANES // head_dim
    v_row = n_kv // pack * s
    row = lax.broadcasted_iota(jnp.int32, (s, s), 0)
    col = lax.broadcasted_iota(jnp.int32, (s, s), 1)
    allowed = jnp.concatenate([row <= col] * groups, axis=1)
    zeros = jnp.zeros((head_dim, groups * s), BF16)
    for g in range(n_kv):
        k_rows = slice(g // pack * s, (g // pack + 1) * s)
        v_rows = slice(v_row + g * head_dim, v_row + (g + 1) * head_dim)
        k_all = jnp.concatenate([r[b, k_rows, :] for r in refs], axis=0)
        v_all = jnp.concatenate([r[b, v_rows, :] for r in refs], axis=1)
        h0 = g * groups
        q = jnp.concatenate([q_ref[b, h * head_dim:(h + 1) * head_dim, :] for h in range(h0, h0 + groups)], axis=1)
        q = jnp.concatenate([q if j == g % pack else zeros for j in range(pack)], axis=0)
        sc = jnp.dot(k_all, q, preferred_element_type=F32)
        full = sc.shape[0] - s
        diag = jnp.where(allowed, sc[full:], -jnp.inf)
        sc = jnp.concatenate([sc[:full], diag], axis=0) if full else diag
        m = jnp.max(sc, axis=0, keepdims=True)
        e = jnp.exp2((sc - m) * factor)
        l = jnp.sum(e, axis=0, keepdims=True)
        o = jnp.dot(v_all, e.astype(BF16), preferred_element_type=F32) / l
        for h in range(0, groups, pack):
            stacked = jnp.concatenate([o[:, (h + j) * s:(h + j + 1) * s] for j in range(pack)], axis=0)
            o_ref[0, :, (h0 + h) * head_dim:(h0 + h + pack) * head_dim] = stacked.astype(BF16).T


def qattn_body(head_dim, n_kv, nq, fchunk, forward_at, n_ref, wq_ref, cos_ref, sin_ref, own, o_ref,
               q_scr, far, swp, near, s_far, r_far, s_swp, r_swp, s_near, r_near):
    i = pl.program_id(0)
    last = pl.num_programs(0) - 1
    me = lax.axis_index("seq")
    n_batch, feats, s = q_scr.shape
    n_chunks = len(forward_at)
    per = n_batch // n_chunks

    def send(src, dst, sems, rems, c, target):
        if c is None:
            return pltpu.make_async_remote_copy(src_ref=src, dst_ref=dst, send_sem=sems.at[0], recv_sem=rems.at[0],
                                                device_id={"seq": target}, device_id_type=pl.DeviceIdType.MESH)
        rows = pl.ds(c * per, per)
        return pltpu.make_async_remote_copy(src_ref=src.at[rows], dst_ref=dst.at[rows], send_sem=sems.at[c], recv_sem=rems.at[c],
                                            device_id={"seq": target}, device_id_type=pl.DeviceIdType.MESH)

    def far_copy(c):
        return send(own, far, s_far, r_far, c, lax.rem(me + 2, 4))

    def swap_copy(c):
        return send(far, swp, s_swp, r_swp, c, 5 - me)

    def near_copy():
        return send(own, near, s_near, r_near, None, me + 1 - 2 * lax.rem(me, 2))

    @pl.when(i == 0)
    def _():
        barrier = pltpu.get_barrier_semaphore()

        def ready(target):
            pl.semaphore_signal(barrier, inc=1, device_id={"seq": target}, device_id_type=pl.DeviceIdType.MESH)

        @pl.when(me == 0)
        def _():
            pl.semaphore_wait(barrier, 2)

        @pl.when(me == 1)
        def _():
            ready(0)
            pl.semaphore_wait(barrier, 1)

        @pl.when(me == 2)
        def _():
            ready(0)
            ready(3)
            pl.semaphore_wait(barrier, 1)

        @pl.when(me == 3)
        def _():
            ready(1)
            ready(2)
            pl.semaphore_wait(barrier, 1)

        @pl.when(me < 2)
        def _():
            for c in range(n_chunks):
                far_copy(c).start()

        @pl.when(lax.rem(me, 2) == 0)
        def _():
            near_copy().start()

    for c, at in enumerate(forward_at):
        @pl.when((i == at) & (me >= 2))
        def _():
            far_copy(c).wait_recv()
            swap_copy(c).start()

        @pl.when((i == nq + c * per) & (me >= 2))
        def _():
            swap_copy(c).wait_recv()

    @pl.when((i == nq) & (lax.rem(me, 2) == 1))
    def _():
        near_copy().wait_recv()

    @pl.when(i < nq)
    def _():
        for f0 in range(0, feats, fchunk):
            u = lax.dot_general(wq_ref[0, f0:f0 + fchunk, :], n_ref[...], NT, preferred_element_type=F32)
            for j in range(n_ref.shape[0] // s):
                for h in range(0, fchunk, head_dim):
                    q_scr[i * (n_ref.shape[0] // s) + j, f0 + h:f0 + h + head_dim, :] = rope_t(
                        u[h:h + head_dim, j * s:(j + 1) * s], cos_ref[...], sin_ref[...])

    sets = ([own], [near, own], [far, swp, own], [far, swp, near, own])
    for dev, refs in enumerate(sets):
        @pl.when((i >= nq) & (me == dev))
        def _():
            attn_one(head_dim, n_kv, q_scr, i - nq, refs, o_ref)

    @pl.when((i == last) & (me < 2))
    def _():
        for c in range(n_chunks):
            far_copy(c).wait_send()

    @pl.when((i == last) & (me >= 2))
    def _():
        for c in range(n_chunks):
            swap_copy(c).wait_send()

    @pl.when((i == last) & (lax.rem(me, 2) == 0))
    def _():
        near_copy().wait_send()


def q_attention(layer, n, wq, cos, sin, own, head_dim, n_kv, tile=256, fchunk=512):
    rows, d = n.shape
    feats = wq.shape[1]
    n_batch, kv_rows, s = own.shape
    nq = rows // tile
    n_chunks = 8
    forward_at = (3, 5, 7) + tuple(nq + 2 * c + 1 for c in range(n_chunks - 3))
    slot = pltpu.VMEM(own.shape, BF16)
    sems = [pltpu.SemaphoreType.DMA((n_chunks,))] * 4 + [pltpu.SemaphoreType.DMA((1,))] * 2
    return pl.pallas_call(
        functools.partial(qattn_body, head_dim, n_kv, nq, fchunk, forward_at),
        grid=(nq + n_batch,),
        in_specs=[
            pl.BlockSpec((tile, d), lambda i: (jnp.minimum(i, nq - 1), 0)),
            pl.BlockSpec((1, feats, d), lambda i: (layer, 0, 0), pipeline_mode=pl.Buffered(1)),
            pl.BlockSpec(cos.shape, lambda i: (0, 0)),
            pl.BlockSpec(cos.shape, lambda i: (0, 0)),
            pl.BlockSpec(own.shape, lambda i: (0, 0, 0), pipeline_mode=pl.Buffered(1)),
        ],
        out_specs=pl.BlockSpec((1, s, feats), lambda i: (jnp.maximum(i - nq, 0), 0, 0)),
        out_shape=jax.ShapeDtypeStruct((n_batch, s, feats), BF16),
        scratch_shapes=[pltpu.VMEM((n_batch, feats, s), BF16), slot, slot, slot] + sems,
        compiler_params=pltpu.CompilerParams(dimension_semantics=("arbitrary",), vmem_limit_bytes=VMEM_LIMIT,
                                             collective_id=layer, has_side_effects=True),
        cost_estimate=cost(2 * rows * d * feats + 4 * rows * feats * 256, 4 * rows * d + 2 * feats * d),
        name="q_attention",
    )(n, wq, cos, sin, own)


def out_body(o_ref, w_ref, x_ref, g_ref, h_ref, r_ref):
    acc = jnp.dot(o_ref[...], w_ref[0], preferred_element_type=F32)
    h = (x_ref[...].astype(F32) + acc).astype(BF16)
    h_ref[...] = h
    r_ref[...] = normed(h, g_ref[0])


def out_proj(layer, o, w, x, gain, tile=256):
    rows, d = x.shape
    k = o.shape[1]
    return pl.pallas_call(
        out_body,
        grid=(rows // tile,),
        in_specs=[
            pl.BlockSpec((tile, k), lambda i: (i, 0)),
            pl.BlockSpec((1, k, d), lambda i: (layer, 0, 0), pipeline_mode=pl.Buffered(1)),
            pl.BlockSpec((tile, d), lambda i: (i, 0)),
            pl.BlockSpec((1, 1, d), lambda i: (layer, 0, 0)),
        ],
        out_specs=[pl.BlockSpec((tile, d), lambda i: (i, 0))] * 2,
        out_shape=[jax.ShapeDtypeStruct((rows, d), BF16)] * 2,
        compiler_params=params(),
        cost_estimate=cost(2 * rows * d * k, 8 * rows * d),
        name="out_proj",
    )(o, w, x, gain)


def mlp_body(n_up, tn, mt, r_ref, wu_ref, wd_ref, h_ref, y_ref, z_ref):
    i = pl.program_id(0)
    rows = r_ref.shape[0]

    @pl.when(i < n_up)
    def _():
        cols = pl.ds(pl.multiple_of(i * tn, tn), tn)
        for m in range(0, rows, mt):
            u = jnp.dot(r_ref[m:m + mt, :], wu_ref[0], preferred_element_type=F32)
            z_ref[m:m + mt, cols] = jax.nn.gelu(u, approximate=True).astype(BF16)

    @pl.when(i >= n_up)
    def _():
        for m in range(0, rows, mt):
            acc = jnp.dot(z_ref[m:m + mt, :], wd_ref[0], preferred_element_type=F32)
            y_ref[m:m + mt, :] = (h_ref[m:m + mt, :].astype(F32) + acc).astype(BF16)


def mlp(layer, r, wu, wd, h, tn=512, td=512, mt=1024):
    rows, d = r.shape
    ff = wu.shape[2]
    n_up = ff // tn
    n_dn = d // td
    return pl.pallas_call(
        functools.partial(mlp_body, n_up, tn, mt),
        grid=(n_up + n_dn,),
        in_specs=[
            pl.BlockSpec((rows, d), lambda i: (0, 0), pipeline_mode=pl.Buffered(1)),
            pl.BlockSpec((1, d, tn), lambda i: (layer, 0, jnp.minimum(i, n_up - 1))),
            pl.BlockSpec((1, ff, td), lambda i: (layer, 0, jnp.maximum(i - n_up, 0))),
            pl.BlockSpec((rows, td), lambda i: (0, jnp.maximum(i - n_up, 0))),
        ],
        out_specs=pl.BlockSpec((rows, td), lambda i: (0, jnp.maximum(i - n_up, 0))),
        out_shape=jax.ShapeDtypeStruct((rows, d), BF16),
        scratch_shapes=[pltpu.VMEM((rows, ff), BF16)],
        compiler_params=params(),
        cost_estimate=cost(4 * rows * d * ff, 4 * ff * d),
        name="mlp",
    )(r, wu, wd, h)


def solution(mesh):
    tok_spec = P(None, ("data", "seq"), None)
    in_specs = (tok_spec, P(("data", "seq"))) + (P(),) * 8

    def device_fn(x_loc, pos_loc, w_query, w_key, w_value, w_out, w_up, w_down, g_attn, g_mlp):
        n_layers, d, n_heads, head_dim = w_query.shape
        n_kv = w_key.shape[2]
        n_batch, s, _ = x_loc.shape
        rows = n_batch * s
        half = head_dim // 2
        inv_freq = ROPE_BASE ** (-jnp.arange(half, dtype=F32) * (2.0 / head_dim))
        angles = inv_freq[:, None] * pos_loc.astype(F32)[None, :]
        cos, sin = jnp.cos(angles), jnp.sin(angles)
        wq = jnp.transpose(w_query, (0, 2, 3, 1)).reshape(n_layers, n_heads * head_dim, d)
        wk = jnp.transpose(w_key, (0, 2, 3, 1)).reshape(n_layers, n_kv * head_dim, d)
        wv = jnp.transpose(w_value, (0, 2, 3, 1)).reshape(n_layers, n_kv * head_dim, d)
        wo = w_out.reshape(n_layers, n_heads * head_dim, d)
        ga = g_attn.reshape(n_layers, 1, d)
        gm = g_mlp.reshape(n_layers, 1, d)
        x = x_loc.reshape(rows, d)
        for layer in range(n_layers):
            n, kv = kv_proj(layer, x, ga, wk, wv, cos, sin, head_dim, n_batch)
            o = q_attention(layer, n, wq, cos, sin, kv, head_dim, n_kv)
            h, r = out_proj(layer, o.reshape(rows, n_heads * head_dim), wo, x, gm)
            x = mlp(layer, r, w_up, w_down, h)
        return x.reshape(x_loc.shape)

    return jax.shard_map(device_fn, mesh=mesh, in_specs=in_specs, out_specs=tok_spec, check_vma=False)
```

time: 988 us -> 719 us (0.73)
  Pallas kernels: 857 us -> 706 us
  waiting for transfers between devices: 91.1 us -> 0 us
  starting transfers between devices: 30.9 us -> 0 us
    pallas_call x6 -> x3, Pallas kernels: 397 us -> 245 us  [q_attention(): pl.pallas_call(functools.partial(qattn_body, head_dim, n_kv, nq, fchunk,...]
    ppermute x18 -> x0, waiting for transfers between devices: 91.1 us -> none  [the longest x6 91.1 us: device_fn(): cross = [lax.ppermute(a, 'seq', ((0, 2), (1, 3))) for a in (k, v)]]
    ppermute x18 -> x0, starting transfers between devices: 30.9 us -> none  [the longest x6 15.4 us: device_fn(): swap = [lax.ppermute(a, 'seq', ((2, 3), (3, 2))) for a in cross]]
  transfers between devices with their start and end apart: 18 -> 0, of which waited for: 6 -> 0; matrix products, arithmetic and copies ran while one was open for 0% -> 0% of each run, Pallas kernels for 7% -> 0%
where the time goes in v2:
time: 719 us; the launch traced here: 710 us
  Pallas kernels  706 us (98%)
    pallas_call x3, Pallas kernels, mlp(): pl.pallas_call(functools.partial(mlp_body, n_up, tn, mt), grid=(n_up + n_...  344 us
    pallas_call x3, Pallas kernels, q_attention(): pl.pallas_call(functools.partial(qattn_body, head_dim, n_kv, nq, fchunk,...  245 us
    pallas_call x3, Pallas kernels, out_proj(): pl.pallas_call(out_body, grid=(rows // tile,), in_specs=[pl.BlockSpec((ti...  80.7 us
    pallas_call x3, Pallas kernels, kv_proj(): pl.pallas_call(functools.partial(kv_body, head_dim, s), grid=(rows // til...  36.5 us

profile of v2, /device:TPU:7, one launch (start us, length us, event | category | flops | bytes accessed | tf_op | source)
XLA Modules:
  0.0 710.3 jit_solution(10247336112363305961)
XLA Ops:
  0.0 0.7 convert_element_type.3
  0.7 1.4 reshape.41.g_ref
  2.1 1.4 reshape.47.g_ref
  3.4 0.7 multiply_sine_fusion
  4.2 12.1 %kv_proj.3 = (bf16[2048,2048]{1,0:T(8,128)(2,1)}, bf16[16,512,128]{2,1,0:T(8,128)(2,1)}) custom-call(bf16[2048,2048]{1,0:T(8,128)(2,1)} %bitcast.21, f32[3,1,2048]{2,1,0:T(1,128)} %reshape.41.g_ref, bf16[3,256,2048]{2,1,0:T(8,128)(2,1)} %bitcast.23, bf16[3,256,2048]{2,1,0:T(8,128)(2,1)} %bitcast.26, f32[32,128]{1,0:T(8,128)} %get-tuple-element.30.cos_ref, ...), custom_call_target="tpu_custom_call" | custom-call | flops 4294967296 | bytes 16777216 | tf_op jit(solution)/shard_map/kv_proj/pallas_call | solution.py:62
  16.3 80.7 %q_attention.3 = bf16[16,128,2048]{2,1,0:T(8,128)(2,1)} custom-call(bf16[2048,2048]{1,0:T(8,128)(2,1)} %get-tuple-element.17.n_ref, bf16[3,2048,2048]{2,1,0:T(8,128)(2,1)} %bitcast.15, f32[32,128]{1,0:T(8,128)} %get-tuple-element.30.cos_ref, f32[32,128]{1,0:T(8,128)} %get-tuple-element.29.sin_ref, bf16[16,512,128]{2,1,0:T(8,128)(2,1)} %get-tuple-element.18.own), custom_call_target="tpu_custom_call" | custom-call | flops 21474836480 | bytes 25165824 | tf_op jit(solution)/shard_map/q_attention/pallas_call | solution.py:234
  97.1 26.9 %out_proj.3 = (bf16[2048,2048]{1,0:T(8,128)(2,1)}, bf16[2048,2048]{1,0:T(8,128)(2,1)}) custom-call(bf16[2048,2048]{1,0:T(8,128)(2,1)} %bitcast.31, bf16[3,2048,2048]{2,1,0:T(8,128)(2,1)} %bitcast.18, bf16[2048,2048]{1,0:T(8,128)(2,1)} %bitcast.22, f32[3,1,2048]{2,1,0:T(1,128)} %reshape.47.g_ref), custom_call_target="tpu_custom_call" | custom-call | flops 17179869184 | bytes 33554432 | tf_op jit(solution)/shard_map/out_proj/pallas_call | solution.py:264
  123.9 114.5 %mlp.3.x_ref = bf16[2048,2048]{1,0:T(8,128)(2,1)} custom-call(bf16[2048,2048]{1,0:T(8,128)(2,1)} %get-tuple-element.19.r_ref, bf16[3,2048,5632]{2,1,0:T(8,128)(2,1)} %wu_ref.5, bf16[3,5632,2048]{2,1,0:T(8,128)(2,1)} %wd_ref.5, bf16[2048,2048]{1,0:T(8,128)(2,1)} %get-tuple-element.20.h_ref), custom_call_target="tpu_custom_call" | custom-call | flops 94489280512 | bytes 46137344 | tf_op jit(solution)/shard_map/mlp/pallas_call | solution.py:304
  238.5 12.2 %kv_proj.4 = (bf16[2048,2048]{1,0:T(8,128)(2,1)}, bf16[16,512,128]{2,1,0:T(8,128)(2,1)}) custom-call(bf16[2048,2048]{1,0:T(8,128)(2,1)} %mlp.3.x_ref, f32[3,1,2048]{2,1,0:T(1,128)} %reshape.41.g_ref, bf16[3,256,2048]{2,1,0:T(8,128)(2,1)} %bitcast.24, bf16[3,256,2048]{2,1,0:T(8,128)(2,1)} %bitcast.27, f32[32,128]{1,0:T(8,128)} %get-tuple-element.30.cos_ref, ...), custom_call_target="tpu_custom_call" | custom-call | flops 4294967296 | bytes 16777216 | tf_op jit(solution)/shard_map/kv_proj/pallas_call | solution.py:62
  250.7 82.2 %q_attention.4 = bf16[16,128,2048]{2,1,0:T(8,128)(2,1)} custom-call(bf16[2048,2048]{1,0:T(8,128)(2,1)} %get-tuple-element.21.n_ref, bf16[3,2048,2048]{2,1,0:T(8,128)(2,1)} %bitcast.16, f32[32,128]{1,0:T(8,128)} %get-tuple-element.30.cos_ref, f32[32,128]{1,0:T(8,128)} %get-tuple-element.29.sin_ref, bf16[16,512,128]{2,1,0:T(8,128)(2,1)} %get-tuple-element.22.own), custom_call_target="tpu_custom_call" | custom-call | flops 21474836480 | bytes 25165824 | tf_op jit(solution)/shard_map/q_attention/pallas_call | solution.py:234
  332.9 26.9 %out_proj.4 = (bf16[2048,2048]{1,0:T(8,128)(2,1)}, bf16[2048,2048]{1,0:T(8,128)(2,1)}) custom-call(bf16[2048,2048]{1,0:T(8,128)(2,1)} %bitcast.30, bf16[3,2048,2048]{2,1,0:T(8,128)(2,1)} %bitcast.19, bf16[2048,2048]{1,0:T(8,128)(2,1)} %mlp.3.x_ref, f32[3,1,2048]{2,1,0:T(1,128)} %reshape.47.g_ref), custom_call_target="tpu_custom_call" | custom-call | flops 17179869184 | bytes 33554432 | tf_op jit(solution)/shard_map/out_proj/pallas_call | solution.py:264
  359.8 114.5 %mlp.4.x_ref = bf16[2048,2048]{1,0:T(8,128)(2,1)} custom-call(bf16[2048,2048]{1,0:T(8,128)(2,1)} %get-tuple-element.23.r_ref, bf16[3,2048,5632]{2,1,0:T(8,128)(2,1)} %wu_ref.5, bf16[3,5632,2048]{2,1,0:T(8,128)(2,1)} %wd_ref.5, bf16[2048,2048]{1,0:T(8,128)(2,1)} %get-tuple-element.24.h_ref), custom_call_target="tpu_custom_call" | custom-call | flops 94489280512 | bytes 46137344 | tf_op jit(solution)/shard_map/mlp/pallas_call | solution.py:304
  474.3 12.2 %kv_proj.5 = (bf16[2048,2048]{1,0:T(8,128)(2,1)}, bf16[16,512,128]{2,1,0:T(8,128)(2,1)}) custom-call(bf16[2048,2048]{1,0:T(8,128)(2,1)} %mlp.4.x_ref, f32[3,1,2048]{2,1,0:T(1,128)} %reshape.41.g_ref, bf16[3,256,2048]{2,1,0:T(8,128)(2,1)} %bitcast.25, bf16[3,256,2048]{2,1,0:T(8,128)(2,1)} %bitcast.28, f32[32,128]{1,0:T(8,128)} %get-tuple-element.30.cos_ref, ...), custom_call_target="tpu_custom_call" | custom-call | flops 4294967296 | bytes 16777216 | tf_op jit(solution)/shard_map/kv_proj/pallas_call | solution.py:62
  486.5 82.0 %q_attention.5 = bf16[16,128,2048]{2,1,0:T(8,128)(2,1)} custom-call(bf16[2048,2048]{1,0:T(8,128)(2,1)} %get-tuple-element.25.n_ref, bf16[3,2048,2048]{2,1,0:T(8,128)(2,1)} %bitcast.17, f32[32,128]{1,0:T(8,128)} %get-tuple-element.30.cos_ref, f32[32,128]{1,0:T(8,128)} %get-tuple-element.29.sin_ref, bf16[16,512,128]{2,1,0:T(8,128)(2,1)} %get-tuple-element.26.own), custom_call_target="tpu_custom_call" | custom-call | flops 21474836480 | bytes 25165824 | tf_op jit(solution)/shard_map/q_attention/pallas_call | solution.py:234
  568.5 26.9 %out_proj.5 = (bf16[2048,2048]{1,0:T(8,128)(2,1)}, bf16[2048,2048]{1,0:T(8,128)(2,1)}) custom-call(bf16[2048,2048]{1,0:T(8,128)(2,1)} %bitcast.29, bf16[3,2048,2048]{2,1,0:T(8,128)(2,1)} %bitcast.20, bf16[2048,2048]{1,0:T(8,128)(2,1)} %mlp.4.x_ref, f32[3,1,2048]{2,1,0:T(1,128)} %reshape.47.g_ref), custom_call_target="tpu_custom_call" | custom-call | flops 17179869184 | bytes 33554432 | tf_op jit(solution)/shard_map/out_proj/pallas_call | solution.py:264
  595.4 114.5 %mlp.5 = bf16[2048,2048]{1,0:T(8,128)(2,1)} custom-call(bf16[2048,2048]{1,0:T(8,128)(2,1)} %get-tuple-element.27.r_ref, bf16[3,2048,5632]{2,1,0:T(8,128)(2,1)} %wu_ref.5, bf16[3,5632,2048]{2,1,0:T(8,128)(2,1)} %wd_ref.5, bf16[2048,2048]{1,0:T(8,128)(2,1)} %get-tuple-element.28.h_ref), custom_call_target="tpu_custom_call" | custom-call | flops 94489280512 | bytes 46137344 | tf_op jit(solution)/shard_map/mlp/pallas_call | solution.py:304
  (1 shorter events, 0.0 us)

commit v3 on v2

--- a/solution.py
+++ b/solution.py
@@ -1,4 +1,5 @@
 import functools
+import math
 
 import jax
 import jax.numpy as jnp
@@ -53,7 +54,7 @@
         kv_ref[i, kv // LANES * batch_rows:, :] = v_t[:, cols]
 
 
-def kv_proj(layer, x, gain, wk, wv, cos, sin, head_dim, n_batch, tile=256):
+def kv_proj(layer, x, gain, wk, wv, cos, sin, head_dim, n_batch, tile=512):
     rows, d = x.shape
     kv = wk.shape[1]
     s = rows // n_batch
@@ -84,39 +85,44 @@
     )(x, gain, wk, wv, cos, sin)
 
 
-def attn_one(head_dim, n_kv, q_ref, b, refs, o_ref):
+def scores(head_dim, n_kv, g, q_ref, b, refs, sc_ref, m_ref):
     s = q_ref.shape[2]
     groups = q_ref.shape[1] // head_dim // n_kv
-    factor = LOG2E * head_dim ** -0.5
     pack = LANES // head_dim
-    v_row = n_kv // pack * s
+    k_rows = slice(g // pack * s, (g // pack + 1) * s)
+    k_all = jnp.concatenate([r[b, k_rows, :] for r in refs], axis=0)
+    h0 = g * groups
+    q = jnp.concatenate([q_ref[b, h * head_dim:(h + 1) * head_dim, :] for h in range(h0, h0 + groups)], axis=1)
+    zeros = jnp.zeros(q.shape, BF16)
+    q = jnp.concatenate([q if j == g % pack else zeros for j in range(pack)], axis=0)
+    sc = jnp.dot(k_all, q, preferred_element_type=F32)
     row = lax.broadcasted_iota(jnp.int32, (s, s), 0)
     col = lax.broadcasted_iota(jnp.int32, (s, s), 1)
     allowed = jnp.concatenate([row <= col] * groups, axis=1)
-    zeros = jnp.zeros((head_dim, groups * s), BF16)
-    for g in range(n_kv):
-        k_rows = slice(g // pack * s, (g // pack + 1) * s)
-        v_rows = slice(v_row + g * head_dim, v_row + (g + 1) * head_dim)
-        k_all = jnp.concatenate([r[b, k_rows, :] for r in refs], axis=0)
-        v_all = jnp.concatenate([r[b, v_rows, :] for r in refs], axis=1)
-        h0 = g * groups
-        q = jnp.concatenate([q_ref[b, h * head_dim:(h + 1) * head_dim, :] for h in range(h0, h0 + groups)], axis=1)
-        q = jnp.concatenate([q if j == g % pack else zeros for j in range(pack)], axis=0)
-        sc = jnp.dot(k_all, q, preferred_element_type=F32)
-        full = sc.shape[0] - s
-        diag = jnp.where(allowed, sc[full:], -jnp.inf)
-        sc = jnp.concatenate([sc[:full], diag], axis=0) if full else diag
-        m = jnp.max(sc, axis=0, keepdims=True)
-        e = jnp.exp2((sc - m) * factor)
-        l = jnp.sum(e, axis=0, keepdims=True)
-        o = jnp.dot(v_all, e.astype(BF16), preferred_element_type=F32) / l
-        for h in range(0, groups, pack):
-            stacked = jnp.concatenate([o[:, (h + j) * s:(h + j + 1) * s] for j in range(pack)], axis=0)
-            o_ref[0, :, (h0 + h) * head_dim:(h0 + h + pack) * head_dim] = stacked.astype(BF16).T
+    full = sc.shape[0] - s
+    diag = jnp.where(allowed, sc[full:], -jnp.inf)
+    sc = jnp.concatenate([sc[:full], diag], axis=0) if full else diag
+    sc_ref[:full + s, :] = sc
+    m_ref[...] = jnp.broadcast_to(jnp.max(sc, axis=0, keepdims=True), m_ref.shape)
+
+
+def combine(head_dim, n_kv, g, b, refs, sc_ref, m_ref, o_ref):
+    s = o_ref.shape[1]
+    groups = o_ref.shape[2] // head_dim // n_kv
+    pack = LANES // head_dim
+    v_row = n_kv // pack * s + g * head_dim
+    v_all = jnp.concatenate([r[b, v_row:v_row + head_dim, :] for r in refs], axis=1)
+    e = jnp.exp2((sc_ref[:len(refs) * s, :] - m_ref[0:1, :]) * (LOG2E * head_dim ** -0.5))
+    l = jnp.sum(e, axis=0, keepdims=True)
+    o = jnp.dot(v_all, e.astype(BF16), preferred_element_type=F32) / l
+    for h in range(0, groups, pack):
+        stacked = jnp.concatenate([o[:, (h + j) * s:(h + j + 1) * s] for j in range(pack)], axis=0)
+        lane = (g * groups + h) * head_dim
+        o_ref[0, :, lane:lane + LANES] = stacked.astype(BF16).T
 
 
 def qattn_body(head_dim, n_kv, nq, fchunk, forward_at, n_ref, wq_ref, cos_ref, sin_ref, own, o_ref,
-               q_scr, far, swp, near, s_far, r_far, s_swp, r_swp, s_near, r_near):
+               q_scr, sc_a, sc_b, m_a, m_b, far, swp, near, s_far, r_far, s_swp, r_swp, s_near, r_near):
     i = pl.program_id(0)
     last = pl.num_programs(0) - 1
     me = lax.axis_index("seq")
@@ -184,7 +190,7 @@
             far_copy(c).wait_recv()
             swap_copy(c).start()
 
-        @pl.when((i == nq + c * per) & (me >= 2))
+        @pl.when((i == nq + max(c * per - 1, 0)) & (me >= 2))
         def _():
             swap_copy(c).wait_recv()
 
@@ -202,10 +208,19 @@
                         u[h:h + head_dim, j * s:(j + 1) * s], cos_ref[...], sin_ref[...])
 
     sets = ([own], [near, own], [far, swp, own], [far, swp, near, own])
+    b = jnp.maximum(i - nq, 0)
+    after = jnp.minimum(b + 1, n_batch - 1)
+    bufs = ((sc_a, m_a), (sc_b, m_b))
     for dev, refs in enumerate(sets):
-        @pl.when((i >= nq) & (me == dev))
-        def _():
-            attn_one(head_dim, n_kv, q_scr, i - nq, refs, o_ref)
+        @pl.when((i == nq) & (me == dev))
+        def _():
+            scores(head_dim, n_kv, 0, q_scr, 0, refs, *bufs[0])
+
+        for g in range(n_kv):
+            @pl.when((i >= nq) & (me == dev))
+            def _():
+                scores(head_dim, n_kv, (g + 1) % n_kv, q_scr, b if g + 1 < n_kv else after, refs, *bufs[(g + 1) % 2])
+                combine(head_dim, n_kv, g, b, refs, *bufs[g % 2], o_ref)
 
     @pl.when((i == last) & (me < 2))
     def _():
@@ -230,6 +245,8 @@
     n_chunks = 8
     forward_at = (3, 5, 7) + tuple(nq + 2 * c + 1 for c in range(n_chunks - 3))
     slot = pltpu.VMEM(own.shape, BF16)
+    wide = feats // head_dim // n_kv * s
+    soft = [pltpu.VMEM((4 * s, wide), F32)] * 2 + [pltpu.VMEM((8, wide), F32)] * 2
     sems = [pltpu.SemaphoreType.DMA((n_chunks,))] * 4 + [pltpu.SemaphoreType.DMA((1,))] * 2
     return pl.pallas_call(
         functools.partial(qattn_body, head_dim, n_kv, nq, fchunk, forward_at),
@@ -243,7 +260,7 @@
         ],
         out_specs=pl.BlockSpec((1, s, feats), lambda i: (jnp.maximum(i - nq, 0), 0, 0)),
         out_shape=jax.ShapeDtypeStruct((n_batch, s, feats), BF16),
-        scratch_shapes=[pltpu.VMEM((n_batch, feats, s), BF16), slot, slot, slot] + sems,
+        scratch_shapes=[pltpu.VMEM((n_batch, feats, s), BF16)] + soft + [slot, slot, slot] + sems,
         compiler_params=pltpu.CompilerParams(dimension_semantics=("arbitrary",), vmem_limit_bytes=VMEM_LIMIT,
                                              collective_id=layer, has_side_effects=True),
         cost_estimate=cost(2 * rows * d * feats + 4 * rows * feats * 256, 4 * rows * d + 2 * feats * d),
@@ -278,6 +295,12 @@
     )(o, w, x, gain)
 
 
+def gelu_tanh(x):
+    root = (2.0 / math.pi) ** 0.5
+    half = 0.5 * x
+    return half + half * jnp.tanh(x * (root + (root * 0.044715) * (x * x)))
+
+
 def mlp_body(n_up, tn, mt, r_ref, wu_ref, wd_ref, h_ref, y_ref, z_ref):
     i = pl.program_id(0)
     rows = r_ref.shape[0]
@@ -287,7 +310,7 @@
         cols = pl.ds(pl.multiple_of(i * tn, tn), tn)
         for m in range(0, rows, mt):
             u = jnp.dot(r_ref[m:m + mt, :], wu_ref[0], preferred_element_type=F32)
-            z_ref[m:m + mt, cols] = jax.nn.gelu(u, approximate=True).astype(BF16)
+            z_ref[m:m + mt, cols] = gelu_tanh(u).astype(BF16)
 
     @pl.when(i >= n_up)
     def _():
@@ -296,7 +319,7 @@
             y_ref[m:m + mt, :] = (h_ref[m:m + mt, :].astype(F32) + acc).astype(BF16)
 
 
-def mlp(layer, r, wu, wd, h, tn=512, td=512, mt=1024):
+def mlp(layer, r, wu, wd, h, tn=512, td=256, mt=1024):
     rows, d = r.shape
     ff = wu.shape[2]
     n_up = ff // tn

time: 719 us -> 674 us (0.937)
  Pallas kernels: 706 us -> 662 us
    pallas_call x3, Pallas kernels: 245 us -> 211 us  [q_attention(): pl.pallas_call(functools.partial(qattn_body, head_dim, n_kv, nq, fchunk,...]
where the time goes in v3:
time: 674 us; the launch traced here: 666 us
  Pallas kernels  662 us (98%)
    pallas_call x3, Pallas kernels, mlp(): pl.pallas_call(functools.partial(mlp_body, n_up, tn, mt), grid=(n_up + n_...  339 us
    pallas_call x3, Pallas kernels, q_attention(): pl.pallas_call(functools.partial(qattn_body, head_dim, n_kv, nq, fchunk,...  211 us
    pallas_call x3, Pallas kernels, out_proj(): pl.pallas_call(out_body, grid=(rows // tile,), in_specs=[pl.BlockSpec((ti...  80.3 us
    pallas_call x3, Pallas kernels, kv_proj(): pl.pallas_call(functools.partial(kv_body, head_dim, s), grid=(rows // til...  31 us

profile of v3, /device:TPU:7, one launch (start us, length us, event | category | flops | bytes accessed | tf_op | source)
XLA Modules:
  0.0 666.2 jit_solution(10401090527714354073)
XLA Ops:
  0.0 0.7 convert_element_type.3
  0.7 1.4 reshape.41.g_ref
  2.1 1.4 reshape.47.g_ref
  3.4 0.7 multiply_sine_fusion
  4.2 10.3 %kv_proj.3 = (bf16[2048,2048]{1,0:T(8,128)(2,1)}, bf16[16,512,128]{2,1,0:T(8,128)(2,1)}) custom-call(bf16[2048,2048]{1,0:T(8,128)(2,1)} %bitcast.21, f32[3,1,2048]{2,1,0:T(1,128)} %reshape.41.g_ref, bf16[3,256,2048]{2,1,0:T(8,128)(2,1)} %bitcast.23, bf16[3,256,2048]{2,1,0:T(8,128)(2,1)} %bitcast.26, f32[32,128]{1,0:T(8,128)} %get-tuple-element.30.cos_ref, ...), custom_call_target="tpu_custom_call" | custom-call | flops 4294967296 | bytes 16777216 | tf_op jit(solution)/shard_map/kv_proj/pallas_call | solution.py:63
  14.5 70.1 %q_attention.3 = bf16[16,128,2048]{2,1,0:T(8,128)(2,1)} custom-call(bf16[2048,2048]{1,0:T(8,128)(2,1)} %get-tuple-element.17.n_ref, bf16[3,2048,2048]{2,1,0:T(8,128)(2,1)} %bitcast.15, f32[32,128]{1,0:T(8,128)} %get-tuple-element.30.cos_ref, f32[32,128]{1,0:T(8,128)} %get-tuple-element.29.sin_ref, bf16[16,512,128]{2,1,0:T(8,128)(2,1)} %get-tuple-element.18.own), custom_call_target="tpu_custom_call" | custom-call | flops 21474836480 | bytes 25165824 | tf_op jit(solution)/shard_map/q_attention/pallas_call | solution.py:251
  84.6 26.8 %out_proj.3 = (bf16[2048,2048]{1,0:T(8,128)(2,1)}, bf16[2048,2048]{1,0:T(8,128)(2,1)}) custom-call(bf16[2048,2048]{1,0:T(8,128)(2,1)} %bitcast.31, bf16[3,2048,2048]{2,1,0:T(8,128)(2,1)} %bitcast.18, bf16[2048,2048]{1,0:T(8,128)(2,1)} %bitcast.22, f32[3,1,2048]{2,1,0:T(1,128)} %reshape.47.g_ref), custom_call_target="tpu_custom_call" | custom-call | flops 17179869184 | bytes 33554432 | tf_op jit(solution)/shard_map/out_proj/pallas_call | solution.py:281
  111.4 112.9 %mlp.3.x_ref = bf16[2048,2048]{1,0:T(8,128)(2,1)} custom-call(bf16[2048,2048]{1,0:T(8,128)(2,1)} %get-tuple-element.19.r_ref, bf16[3,2048,5632]{2,1,0:T(8,128)(2,1)} %wu_ref.5, bf16[3,5632,2048]{2,1,0:T(8,128)(2,1)} %wd_ref.5, bf16[2048,2048]{1,0:T(8,128)(2,1)} %get-tuple-element.20.h_ref), custom_call_target="tpu_custom_call" | custom-call | flops 94489280512 | bytes 46137344 | tf_op jit(solution)/shard_map/mlp/pallas_call | solution.py:327
  224.3 10.3 %kv_proj.4 = (bf16[2048,2048]{1,0:T(8,128)(2,1)}, bf16[16,512,128]{2,1,0:T(8,128)(2,1)}) custom-call(bf16[2048,2048]{1,0:T(8,128)(2,1)} %mlp.3.x_ref, f32[3,1,2048]{2,1,0:T(1,128)} %reshape.41.g_ref, bf16[3,256,2048]{2,1,0:T(8,128)(2,1)} %bitcast.24, bf16[3,256,2048]{2,1,0:T(8,128)(2,1)} %bitcast.27, f32[32,128]{1,0:T(8,128)} %get-tuple-element.30.cos_ref, ...), custom_call_target="tpu_custom_call" | custom-call | flops 4294967296 | bytes 16777216 | tf_op jit(solution)/shard_map/kv_proj/pallas_call | solution.py:63
  234.6 71.0 %q_attention.4 = bf16[16,128,2048]{2,1,0:T(8,128)(2,1)} custom-call(bf16[2048,2048]{1,0:T(8,128)(2,1)} %get-tuple-element.21.n_ref, bf16[3,2048,2048]{2,1,0:T(8,128)(2,1)} %bitcast.16, f32[32,128]{1,0:T(8,128)} %get-tuple-element.30.cos_ref, f32[32,128]{1,0:T(8,128)} %get-tuple-element.29.sin_ref, bf16[16,512,128]{2,1,0:T(8,128)(2,1)} %get-tuple-element.22.own), custom_call_target="tpu_custom_call" | custom-call | flops 21474836480 | bytes 25165824 | tf_op jit(solution)/shard_map/q_attention/pallas_call | solution.py:251
  305.6 26.7 %out_proj.4 = (bf16[2048,2048]{1,0:T(8,128)(2,1)}, bf16[2048,2048]{1,0:T(8,128)(2,1)}) custom-call(bf16[2048,2048]{1,0:T(8,128)(2,1)} %bitcast.30, bf16[3,2048,2048]{2,1,0:T(8,128)(2,1)} %bitcast.19, bf16[2048,2048]{1,0:T(8,128)(2,1)} %mlp.3.x_ref, f32[3,1,2048]{2,1,0:T(1,128)} %reshape.47.g_ref), custom_call_target="tpu_custom_call" | custom-call | flops 17179869184 | bytes 33554432 | tf_op jit(solution)/shard_map/out_proj/pallas_call | solution.py:281
  332.3 113.4 %mlp.4.x_ref = bf16[2048,2048]{1,0:T(8,128)(2,1)} custom-call(bf16[2048,2048]{1,0:T(8,128)(2,1)} %get-tuple-element.23.r_ref, bf16[3,2048,5632]{2,1,0:T(8,128)(2,1)} %wu_ref.5, bf16[3,5632,2048]{2,1,0:T(8,128)(2,1)} %wd_ref.5, bf16[2048,2048]{1,0:T(8,128)(2,1)} %get-tuple-element.24.h_ref), custom_call_target="tpu_custom_call" | custom-call | flops 94489280512 | bytes 46137344 | tf_op jit(solution)/shard_map/mlp/pallas_call | solution.py:327
  445.8 10.3 %kv_proj.5 = (bf16[2048,2048]{1,0:T(8,128)(2,1)}, bf16[16,512,128]{2,1,0:T(8,128)(2,1)}) custom-call(bf16[2048,2048]{1,0:T(8,128)(2,1)} %mlp.4.x_ref, f32[3,1,2048]{2,1,0:T(1,128)} %reshape.41.g_ref, bf16[3,256,2048]{2,1,0:T(8,128)(2,1)} %bitcast.25, bf16[3,256,2048]{2,1,0:T(8,128)(2,1)} %bitcast.28, f32[32,128]{1,0:T(8,128)} %get-tuple-element.30.cos_ref, ...), custom_call_target="tpu_custom_call" | custom-call | flops 4294967296 | bytes 16777216 | tf_op jit(solution)/shard_map/kv_proj/pallas_call | solution.py:63
  456.1 70.2 %q_attention.5 = bf16[16,128,2048]{2,1,0:T(8,128)(2,1)} custom-call(bf16[2048,2048]{1,0:T(8,128)(2,1)} %get-tuple-element.25.n_ref, bf16[3,2048,2048]{2,1,0:T(8,128)(2,1)} %bitcast.17, f32[32,128]{1,0:T(8,128)} %get-tuple-element.30.cos_ref, f32[32,128]{1,0:T(8,128)} %get-tuple-element.29.sin_ref, bf16[16,512,128]{2,1,0:T(8,128)(2,1)} %get-tuple-element.26.own), custom_call_target="tpu_custom_call" | custom-call | flops 21474836480 | bytes 25165824 | tf_op jit(solution)/shard_map/q_attention/pallas_call | solution.py:251
  526.2 26.7 %out_proj.5 = (bf16[2048,2048]{1,0:T(8,128)(2,1)}, bf16[2048,2048]{1,0:T(8,128)(2,1)}) custom-call(bf16[2048,2048]{1,0:T(8,128)(2,1)} %bitcast.29, bf16[3,2048,2048]{2,1,0:T(8,128)(2,1)} %bitcast.20, bf16[2048,2048]{1,0:T(8,128)(2,1)} %mlp.4.x_ref, f32[3,1,2048]{2,1,0:T(1,128)} %reshape.47.g_ref), custom_call_target="tpu_custom_call" | custom-call | flops 17179869184 | bytes 33554432 | tf_op jit(solution)/shard_map/out_proj/pallas_call | solution.py:281
  553.0 113.1 %mlp.5 = bf16[2048,2048]{1,0:T(8,128)(2,1)} custom-call(bf16[2048,2048]{1,0:T(8,128)(2,1)} %get-tuple-element.27.r_ref, bf16[3,2048,5632]{2,1,0:T(8,128)(2,1)} %wu_ref.5, bf16[3,5632,2048]{2,1,0:T(8,128)(2,1)} %wd_ref.5, bf16[2048,2048]{1,0:T(8,128)(2,1)} %get-tuple-element.28.h_ref), custom_call_target="tpu_custom_call" | custom-call | flops 94489280512 | bytes 46137344 | tf_op jit(solution)/shard_map/mlp/pallas_call | solution.py:327
  (1 shorter events, 0.0 us)

commit v4 on v3

--- a/solution.py
+++ b/solution.py
@@ -38,8 +38,8 @@
     return jnp.concatenate([a * cos - b * sin, b * cos + a * sin], axis=0).astype(BF16)
 
 
-def kv_body(head_dim, batch_rows, x_ref, g_ref, wk_ref, wv_ref, cos_ref, sin_ref, n_ref, kv_ref):
-    n = normed(x_ref[...], g_ref[0])
+def kv_body(layer, head_dim, batch_rows, x_ref, g_ref, wk_ref, wv_ref, cos_ref, sin_ref, n_ref, kv_ref):
+    n = normed(x_ref[...], g_ref[layer:layer + 1, :])
     n_ref[...] = n
     k_t = lax.dot_general(wk_ref[0], n, NT, preferred_element_type=F32)
     v_t = lax.dot_general(wv_ref[0], n, NT, preferred_element_type=F32).astype(BF16)
@@ -61,11 +61,11 @@
     per = tile // s
     kv_rows = kv // LANES * s + kv
     return pl.pallas_call(
-        functools.partial(kv_body, head_dim, s),
+        functools.partial(kv_body, layer, head_dim, s),
         grid=(rows // tile,),
         in_specs=[
             pl.BlockSpec((tile, d), lambda i: (i, 0)),
-            pl.BlockSpec((1, 1, d), lambda i: (layer, 0, 0)),
+            pl.BlockSpec(gain.shape, lambda i: (0, 0)),
             pl.BlockSpec((1, kv, d), lambda i: (layer, 0, 0)),
             pl.BlockSpec((1, kv, d), lambda i: (layer, 0, 0)),
             pl.BlockSpec(cos.shape, lambda i: (0, 0)),
@@ -121,8 +121,8 @@
         o_ref[0, :, lane:lane + LANES] = stacked.astype(BF16).T
 
 
-def qattn_body(head_dim, n_kv, nq, fchunk, forward_at, n_ref, wq_ref, cos_ref, sin_ref, own, o_ref,
-               q_scr, sc_a, sc_b, m_a, m_b, far, swp, near, s_far, r_far, s_swp, r_swp, s_near, r_near):
+def qattn_body(layer, head_dim, n_kv, nq, fchunk, forward_at, n_ref, wq_ref, cos_ref, sin_ref, own, o_ref,
+               q_scr, w_scr, w_sem, sc_a, sc_b, m_a, m_b, far, swp, near, s_far, r_far, s_swp, r_swp, s_near, r_near):
     i = pl.program_id(0)
     last = pl.num_programs(0) - 1
     me = lax.axis_index("seq")
@@ -147,8 +147,14 @@
     def near_copy():
         return send(own, near, s_near, r_near, None, me + 1 - 2 * lax.rem(me, 2))
 
+    def weight_copy(c):
+        part = slice(c * fchunk, (c + 1) * fchunk)
+        return pltpu.make_async_copy(wq_ref.at[layer, part, :], w_scr.at[part, :], w_sem.at[c])
+
     @pl.when(i == 0)
     def _():
+        for c in range(feats // fchunk):
+            weight_copy(c).start()
         barrier = pltpu.get_barrier_semaphore()
 
         def ready(target):
@@ -198,14 +204,23 @@
     def _():
         near_copy().wait_recv()
 
-    @pl.when(i < nq)
+    def project(f0):
+        u = lax.dot_general(w_scr[f0:f0 + fchunk, :], n_ref[...], NT, preferred_element_type=F32)
+        for j in range(n_ref.shape[0] // s):
+            for h in range(0, fchunk, head_dim):
+                q_scr[i * (n_ref.shape[0] // s) + j, f0 + h:f0 + h + head_dim, :] = rope_t(
+                    u[h:h + head_dim, j * s:(j + 1) * s], cos_ref[...], sin_ref[...])
+
+    @pl.when(i == 0)
+    def _():
+        for c, f0 in enumerate(range(0, feats, fchunk)):
+            weight_copy(c).wait()
+            project(f0)
+
+    @pl.when((i > 0) & (i < nq))
     def _():
         for f0 in range(0, feats, fchunk):
-            u = lax.dot_general(wq_ref[0, f0:f0 + fchunk, :], n_ref[...], NT, preferred_element_type=F32)
-            for j in range(n_ref.shape[0] // s):
-                for h in range(0, fchunk, head_dim):
-                    q_scr[i * (n_ref.shape[0] // s) + j, f0 + h:f0 + h + head_dim, :] = rope_t(
-                        u[h:h + head_dim, j * s:(j + 1) * s], cos_ref[...], sin_ref[...])
+            project(f0)
 
     sets = ([own], [near, own], [far, swp, own], [far, swp, near, own])
     b = jnp.maximum(i - nq, 0)
@@ -249,18 +264,19 @@
     soft = [pltpu.VMEM((4 * s, wide), F32)] * 2 + [pltpu.VMEM((8, wide), F32)] * 2
     sems = [pltpu.SemaphoreType.DMA((n_chunks,))] * 4 + [pltpu.SemaphoreType.DMA((1,))] * 2
     return pl.pallas_call(
-        functools.partial(qattn_body, head_dim, n_kv, nq, fchunk, forward_at),
+        functools.partial(qattn_body, layer, head_dim, n_kv, nq, fchunk, forward_at),
         grid=(nq + n_batch,),
         in_specs=[
             pl.BlockSpec((tile, d), lambda i: (jnp.minimum(i, nq - 1), 0)),
-            pl.BlockSpec((1, feats, d), lambda i: (layer, 0, 0), pipeline_mode=pl.Buffered(1)),
+            pl.BlockSpec(memory_space=pl.ANY),
             pl.BlockSpec(cos.shape, lambda i: (0, 0)),
             pl.BlockSpec(cos.shape, lambda i: (0, 0)),
             pl.BlockSpec(own.shape, lambda i: (0, 0, 0), pipeline_mode=pl.Buffered(1)),
         ],
         out_specs=pl.BlockSpec((1, s, feats), lambda i: (jnp.maximum(i - nq, 0), 0, 0)),
         out_shape=jax.ShapeDtypeStruct((n_batch, s, feats), BF16),
-        scratch_shapes=[pltpu.VMEM((n_batch, feats, s), BF16)] + soft + [slot, slot, slot] + sems,
+        scratch_shapes=[pltpu.VMEM((n_batch, feats, s), BF16), pltpu.VMEM((feats, d), BF16),
+                        pltpu.SemaphoreType.DMA((feats // fchunk,))] + soft + [slot, slot, slot] + sems,
         compiler_params=pltpu.CompilerParams(dimension_semantics=("arbitrary",), vmem_limit_bytes=VMEM_LIMIT,
                                              collective_id=layer, has_side_effects=True),
         cost_estimate=cost(2 * rows * d * feats + 4 * rows * feats * 256, 4 * rows * d + 2 * feats * d),
@@ -268,24 +284,24 @@
     )(n, wq, cos, sin, own)
 
 
-def out_body(o_ref, w_ref, x_ref, g_ref, h_ref, r_ref):
+def out_body(layer, o_ref, w_ref, x_ref, g_ref, h_ref, r_ref):
     acc = jnp.dot(o_ref[...], w_ref[0], preferred_element_type=F32)
     h = (x_ref[...].astype(F32) + acc).astype(BF16)
     h_ref[...] = h
-    r_ref[...] = normed(h, g_ref[0])
+    r_ref[...] = normed(h, g_ref[layer:layer + 1, :])
 
 
 def out_proj(layer, o, w, x, gain, tile=256):
     rows, d = x.shape
     k = o.shape[1]
     return pl.pallas_call(
-        out_body,
+        functools.partial(out_body, layer),
         grid=(rows // tile,),
         in_specs=[
             pl.BlockSpec((tile, k), lambda i: (i, 0)),
             pl.BlockSpec((1, k, d), lambda i: (layer, 0, 0), pipeline_mode=pl.Buffered(1)),
             pl.BlockSpec((tile, d), lambda i: (i, 0)),
-            pl.BlockSpec((1, 1, d), lambda i: (layer, 0, 0)),
+            pl.BlockSpec(gain.shape, lambda i: (0, 0)),
         ],
         out_specs=[pl.BlockSpec((tile, d), lambda i: (i, 0))] * 2,
         out_shape=[jax.ShapeDtypeStruct((rows, d), BF16)] * 2,
@@ -359,13 +375,11 @@
         wk = jnp.transpose(w_key, (0, 2, 3, 1)).reshape(n_layers, n_kv * head_dim, d)
         wv = jnp.transpose(w_value, (0, 2, 3, 1)).reshape(n_layers, n_kv * head_dim, d)
         wo = w_out.reshape(n_layers, n_heads * head_dim, d)
-        ga = g_attn.reshape(n_layers, 1, d)
-        gm = g_mlp.reshape(n_layers, 1, d)
         x = x_loc.reshape(rows, d)
         for layer in range(n_layers):
-            n, kv = kv_proj(layer, x, ga, wk, wv, cos, sin, head_dim, n_batch)
+            n, kv = kv_proj(layer, x, g_attn, wk, wv, cos, sin, head_dim, n_batch)
             o = q_attention(layer, n, wq, cos, sin, kv, head_dim, n_kv)
-            h, r = out_proj(layer, o.reshape(rows, n_heads * head_dim), wo, x, gm)
+            h, r = out_proj(layer, o.reshape(rows, n_heads * head_dim), wo, x, g_mlp)
             x = mlp(layer, r, w_up, w_down, h)
         return x.reshape(x_loc.shape)
 

time: 674 us -> 671 us (level)
  no operation moved by 1% of the time
where the time goes in v4:
time: 671 us; the launch traced here: 662 us
  Pallas kernels  660 us (98%)
    pallas_call x3, Pallas kernels, mlp(): pl.pallas_call(functools.partial(mlp_body, n_up, tn, mt), grid=(n_up + n_...  339 us
    pallas_call x3, Pallas kernels, q_attention(): pl.pallas_call(functools.partial(qattn_body, layer, head_dim, n_kv, nq, f...  210 us
    pallas_call x3, Pallas kernels, out_proj(): pl.pallas_call(functools.partial(out_body, layer), grid=(rows // tile,),...  80.6 us
    pallas_call x3, Pallas kernels, kv_proj(): pl.pallas_call(functools.partial(kv_body, layer, head_dim, s), grid=(rows...  31 us

profile of v4, /device:TPU:7, one launch (start us, length us, event | category | flops | bytes accessed | tf_op | source)
XLA Modules:
  0.0 661.9 jit_solution(6547474883916370838)
XLA Ops:
  0.0 0.7 convert_element_type.3
  0.7 0.8 multiply_sine_fusion
  1.4 10.3 %kv_proj.3 = (bf16[2048,2048]{1,0:T(8,128)(2,1)}, bf16[16,512,128]{2,1,0:T(8,128)(2,1)}) custom-call(bf16[2048,2048]{1,0:T(8,128)(2,1)} %bitcast.21, f32[3,2048]{1,0:T(4,128)} %g_ref.10, bf16[3,256,2048]{2,1,0:T(8,128)(2,1)} %bitcast.23, bf16[3,256,2048]{2,1,0:T(8,128)(2,1)} %bitcast.26, f32[32,128]{1,0:T(8,128)} %get-tuple-element.30.cos_ref, ...), custom_call_target="tpu_custom_call" | custom-call | flops 4294967296 | bytes 16777216 | tf_op jit(solution)/shard_map/kv_proj/pallas_call | solution.py:63
  11.7 69.7 %q_attention.3 = bf16[16,128,2048]{2,1,0:T(8,128)(2,1)} custom-call(bf16[2048,2048]{1,0:T(8,128)(2,1)} %get-tuple-element.17.n_ref, bf16[3,2048,2048]{2,1,0:T(8,128)(2,1)} %bitcast.15, f32[32,128]{1,0:T(8,128)} %get-tuple-element.30.cos_ref, f32[32,128]{1,0:T(8,128)} %get-tuple-element.29.sin_ref, bf16[16,512,128]{2,1,0:T(8,128)(2,1)} %get-tuple-element.18.own), custom_call_target="tpu_custom_call" | custom-call | flops 21474836480 | bytes 25165824 | tf_op jit(solution)/shard_map/q_attention/pallas_call | solution.py:266
  81.5 26.9 %out_proj.3 = (bf16[2048,2048]{1,0:T(8,128)(2,1)}, bf16[2048,2048]{1,0:T(8,128)(2,1)}) custom-call(bf16[2048,2048]{1,0:T(8,128)(2,1)} %bitcast.31, bf16[3,2048,2048]{2,1,0:T(8,128)(2,1)} %bitcast.18, bf16[2048,2048]{1,0:T(8,128)(2,1)} %bitcast.22, f32[3,2048]{1,0:T(4,128)} %g_ref.11), custom_call_target="tpu_custom_call" | custom-call | flops 17179869184 | bytes 33554432 | tf_op jit(solution)/shard_map/out_proj/pallas_call | solution.py:297
  108.3 112.9 %mlp.3.x_ref = bf16[2048,2048]{1,0:T(8,128)(2,1)} custom-call(bf16[2048,2048]{1,0:T(8,128)(2,1)} %get-tuple-element.19.r_ref, bf16[3,2048,5632]{2,1,0:T(8,128)(2,1)} %wu_ref.5, bf16[3,5632,2048]{2,1,0:T(8,128)(2,1)} %wd_ref.5, bf16[2048,2048]{1,0:T(8,128)(2,1)} %get-tuple-element.20.h_ref), custom_call_target="tpu_custom_call" | custom-call | flops 94489280512 | bytes 46137344 | tf_op jit(solution)/shard_map/mlp/pallas_call | solution.py:343
  221.3 10.3 %kv_proj.4 = (bf16[2048,2048]{1,0:T(8,128)(2,1)}, bf16[16,512,128]{2,1,0:T(8,128)(2,1)}) custom-call(bf16[2048,2048]{1,0:T(8,128)(2,1)} %mlp.3.x_ref, f32[3,2048]{1,0:T(4,128)} %g_ref.10, bf16[3,256,2048]{2,1,0:T(8,128)(2,1)} %bitcast.24, bf16[3,256,2048]{2,1,0:T(8,128)(2,1)} %bitcast.27, f32[32,128]{1,0:T(8,128)} %get-tuple-element.30.cos_ref, ...), custom_call_target="tpu_custom_call" | custom-call | flops 4294967296 | bytes 16777216 | tf_op jit(solution)/shard_map/kv_proj/pallas_call | solution.py:63
  231.6 70.1 %q_attention.4 = bf16[16,128,2048]{2,1,0:T(8,128)(2,1)} custom-call(bf16[2048,2048]{1,0:T(8,128)(2,1)} %get-tuple-element.21.n_ref, bf16[3,2048,2048]{2,1,0:T(8,128)(2,1)} %bitcast.16, f32[32,128]{1,0:T(8,128)} %get-tuple-element.30.cos_ref, f32[32,128]{1,0:T(8,128)} %get-tuple-element.29.sin_ref, bf16[16,512,128]{2,1,0:T(8,128)(2,1)} %get-tuple-element.22.own), custom_call_target="tpu_custom_call" | custom-call | flops 21474836480 | bytes 25165824 | tf_op jit(solution)/shard_map/q_attention/pallas_call | solution.py:266
  301.7 26.8 %out_proj.4 = (bf16[2048,2048]{1,0:T(8,128)(2,1)}, bf16[2048,2048]{1,0:T(8,128)(2,1)}) custom-call(bf16[2048,2048]{1,0:T(8,128)(2,1)} %bitcast.30, bf16[3,2048,2048]{2,1,0:T(8,128)(2,1)} %bitcast.19, bf16[2048,2048]{1,0:T(8,128)(2,1)} %mlp.3.x_ref, f32[3,2048]{1,0:T(4,128)} %g_ref.11), custom_call_target="tpu_custom_call" | custom-call | flops 17179869184 | bytes 33554432 | tf_op jit(solution)/shard_map/out_proj/pallas_call | solution.py:297
  328.6 112.9 %mlp.4.x_ref = bf16[2048,2048]{1,0:T(8,128)(2,1)} custom-call(bf16[2048,2048]{1,0:T(8,128)(2,1)} %get-tuple-element.23.r_ref, bf16[3,2048,5632]{2,1,0:T(8,128)(2,1)} %wu_ref.5, bf16[3,5632,2048]{2,1,0:T(8,128)(2,1)} %wd_ref.5, bf16[2048,2048]{1,0:T(8,128)(2,1)} %get-tuple-element.24.h_ref), custom_call_target="tpu_custom_call" | custom-call | flops 94489280512 | bytes 46137344 | tf_op jit(solution)/shard_map/mlp/pallas_call | solution.py:343
  441.5 10.3 %kv_proj.5 = (bf16[2048,2048]{1,0:T(8,128)(2,1)}, bf16[16,512,128]{2,1,0:T(8,128)(2,1)}) custom-call(bf16[2048,2048]{1,0:T(8,128)(2,1)} %mlp.4.x_ref, f32[3,2048]{1,0:T(4,128)} %g_ref.10, bf16[3,256,2048]{2,1,0:T(8,128)(2,1)} %bitcast.25, bf16[3,256,2048]{2,1,0:T(8,128)(2,1)} %bitcast.28, f32[32,128]{1,0:T(8,128)} %get-tuple-element.30.cos_ref, ...), custom_call_target="tpu_custom_call" | custom-call | flops 4294967296 | bytes 16777216 | tf_op jit(solution)/shard_map/kv_proj/pallas_call | solution.py:63
  451.8 69.9 %q_attention.5 = bf16[16,128,2048]{2,1,0:T(8,128)(2,1)} custom-call(bf16[2048,2048]{1,0:T(8,128)(2,1)} %get-tuple-element.25.n_ref, bf16[3,2048,2048]{2,1,0:T(8,128)(2,1)} %bitcast.17, f32[32,128]{1,0:T(8,128)} %get-tuple-element.30.cos_ref, f32[32,128]{1,0:T(8,128)} %get-tuple-element.29.sin_ref, bf16[16,512,128]{2,1,0:T(8,128)(2,1)} %get-tuple-element.26.own), custom_call_target="tpu_custom_call" | custom-call | flops 21474836480 | bytes 25165824 | tf_op jit(solution)/shard_map/q_attention/pallas_call | solution.py:266
  521.8 26.9 %out_proj.5 = (bf16[2048,2048]{1,0:T(8,128)(2,1)}, bf16[2048,2048]{1,0:T(8,128)(2,1)}) custom-call(bf16[2048,2048]{1,0:T(8,128)(2,1)} %bitcast.29, bf16[3,2048,2048]{2,1,0:T(8,128)(2,1)} %bitcast.20, bf16[2048,2048]{1,0:T(8,128)(2,1)} %mlp.4.x_ref, f32[3,2048]{1,0:T(4,128)} %g_ref.11), custom_call_target="tpu_custom_call" | custom-call | flops 17179869184 | bytes 33554432 | tf_op jit(solution)/shard_map/out_proj/pallas_call | solution.py:297
  548.7 112.8 %mlp.5 = bf16[2048,2048]{1,0:T(8,128)(2,1)} custom-call(bf16[2048,2048]{1,0:T(8,128)(2,1)} %get-tuple-element.27.r_ref, bf16[3,2048,5632]{2,1,0:T(8,128)(2,1)} %wu_ref.5, bf16[3,5632,2048]{2,1,0:T(8,128)(2,1)} %wd_ref.5, bf16[2048,2048]{1,0:T(8,128)(2,1)} %get-tuple-element.28.h_ref), custom_call_target="tpu_custom_call" | custom-call | flops 94489280512 | bytes 46137344 | tf_op jit(solution)/shard_map/mlp/pallas_call | solution.py:343
  (1 shorter events, 0.0 us)
